TPU v7x, 128 devices: a whole 4x4x4 slice. The times are simulated.
128 devices in a mesh: gx: 8 (over y, core), gy: 16 (over x, z).
Axes of the slice: x: 4, y: 4, z: 4, core: 2. Of those that a mesh axis runs over, the one named last changes fastest.
Arguments:
- disp: float32 [3, 64, 256, 128], P(None, 'gx', 'gy'), may hold values from -3 to 3
- vel: float32 [3, 64, 256, 128], P(None, 'gx', 'gy'), may hold values from -30 to 30
- load: float32 [3, 64, 256, 128], P(None, 'gx', 'gy'), may hold values from -96 to 96
- flags: int32 [64, 256, 128], P('gx', 'gy'), may hold values 0 or 1
- mask_bits: int32 [4, 64, 256, 128], P(None, 'gx', 'gy'), may hold values from 0 to 2147483647, as said below
Outputs:
- disp_out: float32 [3, 64, 256, 128], P(None, 'gx', 'gy')
- vel_out: float32 [3, 64, 256, 128], P(None, 'gx', 'gy')
Inputs may be any that keep to these rules, and one draw needn't show every extreme that they name: `mask_bits`: bit b (0 to 30) of word w marks the cell's bond to neighbour number 31 w + b as broken; bit 31, and bits of numbers 122 and above, are zero.
All inputs are finite; a program needn't handle non-finite values. No bound on the sum of `flags` on one device may be relied on, other than what follows from the above.
Results may differ from a plain program's by a relative error of at most 0.0001.
Values sent between devices are 32-bit elements; how exact they have to be, the bound alone decides.
A program may use at most 128 MiB of HBM per device.

v0:
```python
import functools
import math

import jax
import jax.numpy as jnp
from jax import lax
from jax.experimental import pallas as pl
from jax.experimental.pallas import tpu as pltpu
from jax.sharding import PartitionSpec as P

ITERS = 8
MASS = 64.0
EPSILON = 1e-06
ROWS = 8
COLS = 16
DEPTH = 128
PAD = 8
WIDE = COLS + 2 * PAD
TALL = ROWS + 6
GROUP = 4
SLOTS = 4
F32 = jnp.float32
I32 = jnp.int32


def neighbour_table():
    table = []
    for across in range(-3, 4):
        for along in range(-3, 4):
            for upward in range(-3, 4):
                length = across * across + along * along + upward * upward
                if 0 < length <= 9:
                    table.append((across, along, upward))
    return table


TABLE = neighbour_table()
NUMBER = {offset: k for k, offset in enumerate(TABLE)}
BONDS = len(TABLE)


def on_axis(offset):
    return sum(1 for part in offset if part) == 1


def weight_of(offset):
    length = float(sum(part * part for part in offset))
    weight = 1.0 / (length * math.sqrt(length))
    return weight * length if on_axis(offset) else weight


def oblique(b, c):
    return [a for a in range(-2, 3) if (a, b, c) in NUMBER and not on_axis((a, b, c))]


EDGE = []
for _c in range(-2, 3):
    for _reach in (1, 2, 3):
        for _a in range(-2, 3):
            if (_a, _reach, _c) in NUMBER:
                for _j in range(_reach):
                    EDGE.append((_a, _reach, _c, _j, _reach - 1 - _j))
EDGE_AT = {entry[:4]: n for n, entry in enumerate(EDGE)}


def add(total, term):
    return term if total is None else total + term


def sub(total, term):
    return -term if total is None else total - term


def scaled(factor, value):
    if factor == 1:
        return value
    if factor == -1:
        return -value
    return float(factor) * value


def plus_scaled(total, factor, value):
    if total is None:
        return scaled(factor, value)
    if factor == 1:
        return total + value
    if factor == -1:
        return total - value
    return total + float(factor) * value


def combine(weights, totals):
    out = None
    for factor, value in zip(weights, totals):
        if factor and value is not None:
            out = plus_scaled(out, factor, value)
    return out


def turned(value, c):
    if c == 0:
        return value
    return pltpu.roll(value, (-c) % DEPTH, 1)


def moments(terms):
    zeroth = None
    for a in sorted(terms):
        zeroth = add(zeroth, terms[a])
    first = None
    if 2 in terms:
        first = add(first, terms[2])
    if -2 in terms:
        first = sub(first, terms[-2])
    if first is not None:
        first = 2.0 * first
    if 1 in terms:
        first = add(first, terms[1])
    if -1 in terms:
        first = sub(first, terms[-1])
    return zeroth, first


def local_pass(slot, field, bond, diag, out):
    def group(g, carry):
        base = g * GROUP
        for t in range(2):
            col = PAD + 8 * t

            def coef(offset, i):
                start = pl.multiple_of((base + i) * COLS + 8 * t, 8)
                return bond[NUMBER[offset], pl.ds(start, 8), :]

            def source(part, i, b):
                return field[slot, part, base + 3 + i, pl.ds(col + b, 8), :]

            for c in (0, 1, -1, 2, -2, 3, -3):
                g0 = [None] * GROUP
                g1 = [None] * GROUP
                g2 = [None] * GROUP
                if c:
                    for i in range(GROUP):
                        g2[i] = coef((0, 0, c), i) * source(2, i, 0)
                if c == 0:
                    for i in range(GROUP):
                        for a in (1, -1, 2, -2, 3, -3):
                            g0[i] = add(g0[i], coef((a, 0, 0), i) * source(0, i + a, 0))
                        for b in (1, -1, 2, -2, 3, -3):
                            g1[i] = add(g1[i], coef((0, b, 0), i) * source(1, i, b))
                if abs(c) < 3:
                    n0 = [None] * GROUP
                    n1 = [None] * GROUP
                    for b in (2, -2, 1, -1, 0):
                        reach = oblique(b, c)
                        if not reach:
                            continue
                        span = range(min(reach), GROUP + max(reach))
                        u0 = {i: source(0, i, b) for i in span}
                        twice = {i: 2.0 * u0[i] for i in span} if 2 in reach else None
                        u1 = {i: source(1, i, b) if b else None for i in span}
                        u2 = {i: source(2, i, b) if c else None for i in span}
                        s = {i: combine((b, c), (u1[i], u2[i])) for i in span}
                        for i in range(GROUP):
                            terms = {}
                            for a in reach:
                                near = s[i + a]
                                if abs(a) == 1:
                                    near = near + u0[i + a] if a > 0 else near - u0[i + a]
                                elif a:
                                    near = near + twice[i + a] if a > 0 else near - twice[i + a]
                                terms[a] = coef((a, b, c), i) * near
                            zeroth, first = moments(terms)
                            g0[i] = add(g0[i], first)
                            if c:
                                n0[i] = add(n0[i], zeroth)
                            if b == 2:
                                n1[i] = zeroth
                            elif b == -2:
                                n1[i] = 2.0 * (n1[i] - zeroth)
                            elif b:
                                n1[i] = plus_scaled(n1[i], b, zeroth)
                    for i in range(GROUP):
                        g1[i] = add(g1[i], n1[i])
                        if c:
                            g2[i] = plus_scaled(g2[i], c, n0[i])
                for i in range(GROUP):
                    for part, value in enumerate((g0[i], g1[i], g2[i])):
                        if c == 0:
                            u = [source(other, i, 0) for other in range(3)]
                            own = None
                            for other in range(3):
                                pair = DIAG[min(part, other), max(part, other)]
                                own = add(own, diag[pair, base + i, pl.ds(8 * t, 8), :] * u[other])
                            value = -own if value is None else value - own
                            out[part, base + i, pl.ds(8 * t, 8), :] = value
                        elif value is not None:
                            out[part, base + i, pl.ds(8 * t, 8), :] += turned(value, c)
        return carry

    lax.fori_loop(0, ROWS // GROUP, group, 0)


DIAG = {(0, 0): 0, (0, 1): 1, (1, 1): 2, (0, 2): 3, (1, 2): 4, (2, 2): 5}


def across_pass(slot, near, far, bond, out):
    for side in range(2):
        sign = 1 if side else -1
        edge = ROWS - 1 if side else 0
        for t in range(2):
            col = PAD + 8 * t

            def coef(offset, i):
                return bond[NUMBER[offset], pl.ds((edge - sign * i) * COLS + 8 * t, 8), :]

            def source(part, layer, b):
                e = layer if side else 1 - layer
                return near[slot, side, part, e, pl.ds(col + b, 8), :]

            sums = [[None] * 3 for i in range(2)]
            third = None
            for c in (0, 1, -1, 2, -2):
                g = [[None] * 3 for i in range(2)]
                if c == 0:
                    for layer in range(2):
                        u0 = source(0, layer, 0)
                        for i in range(3):
                            a = sign * (i + layer + 1)
                            if abs(a) <= 3:
                                term = coef((a, 0, 0), i) * u0
                                if i < 2:
                                    g[i][0] = add(g[i][0], term)
                                else:
                                    third = term
                    g[0][0] = g[0][0] + coef((3 * sign, 0, 0), 0) * far[slot, side, pl.ds(col, 8), :]
                n0 = [None] * 2
                n1 = [None] * 2
                for b in (2, -2, 1, -1, 0):
                    reach = oblique(b, c)
                    if not reach:
                        continue
                    zeroth = [None] * 2
                    deep = [None] * 2
                    for layer in range(max(reach)):
                        u0 = source(0, layer, b)
                        u1 = source(1, layer, b) if b else None
                        u2 = source(2, layer, b) if c else None
                        s = combine((b, c), (u1, u2))
                        for i in range(2):
                            size = i + layer + 1
                            a = sign * size
                            if a in reach:
                                q = plus_scaled(s, a, u0)
                                term = coef((a, b, c), i) * q
                                zeroth[i] = add(zeroth[i], term)
                                if size == 1:
                                    g[i][0] = plus_scaled(g[i][0], sign, term)
                                else:
                                    deep[i] = add(deep[i], term)
                    for i in range(2):
                        if deep[i] is not None:
                            g[i][0] = plus_scaled(g[i][0], 2 * sign, deep[i])
                        if zeroth[i] is None:
                            continue
                        if c:
                            n0[i] = add(n0[i], zeroth[i])
                        if b:
                            n1[i] = plus_scaled(n1[i], b, zeroth[i])
                for i in range(2):
                    g[i][1] = n1[i]
                    g[i][2] = scaled(c, n0[i]) if c else None
                    for part in range(3):
                        if g[i][part] is not None:
                            sums[i][part] = add(sums[i][part], turned(g[i][part], c))
            for i in range(2):
                row = edge - sign * i
                for part in range(3):
                    out[part, row, pl.ds(8 * t, 8), :] += sums[i][part]
            out[0, edge - 2 * sign, pl.ds(8 * t, 8), :] += third


def along_pass(slot, rim, bond_edge, out):
    for side in range(2):
        sign = 1 if side else -1
        edge = COLS - 1 if side else 0

        def coef(a, size, c, j):
            return bond_edge[side, EDGE_AT[a, size, c, j]]

        def source(part, layer, a):
            return rim[slot, side, part * 2 + layer, pl.ds(8 + a, 8), :]

        sums = [[None] * 3 for j in range(2)]
        third = None
        for c in (0, 1, -1, 2, -2):
            g = [[None] * 3 for j in range(2)]
            if c == 0:
                for layer in range(3):
                    at = 6 if layer == 2 else 2 + layer
                    u1 = rim[slot, side, at, pl.ds(8, 8), :]
                    for j in range(3 - layer):
                        term = coef(0, layer + 1 + j, 0, j) * u1
                        if j < 2:
                            g[j][1] = add(g[j][1], term)
                        else:
                            third = term
            n0 = [None] * 2
            n1 = [None] * 2
            for a in (2, -2, 1, -1, 0):
                reach = [size for size in (1, 2) if (a, size, c) in NUMBER and not on_axis((a, size, c))]
                if not reach:
                    continue
                zeroth = [None] * 2
                deep = [None] * 2
                for layer in range(max(reach)):
                    u0 = source(0, layer, a) if a else None
                    u1 = source(1, layer, a)
                    u2 = source(2, layer, a) if c else None
                    s = combine((a, c), (u0, u2))
                    for j in range(2):
                        size = j + layer + 1
                        if size in reach:
                            term = coef(a, size, c, j) * plus_scaled(s, sign * size, u1)
                            zeroth[j] = add(zeroth[j], term)
                            if size == 1:
                                g[j][1] = plus_scaled(g[j][1], sign, term)
                            else:
                                deep[j] = add(deep[j], term)
                for j in range(2):
                    if deep[j] is not None:
                        g[j][1] = plus_scaled(g[j][1], 2 * sign, deep[j])
                    if zeroth[j] is None:
                        continue
                    if c:
                        n0[j] = add(n0[j], zeroth[j])
                    if a:
                        n1[j] = plus_scaled(n1[j], a, zeroth[j])
            for j in range(2):
                g[j][0] = n1[j]
                g[j][2] = scaled(c, n0[j]) if c else None
                for part in range(3):
                    if g[j][part] is not None:
                        sums[j][part] = add(sums[j][part], turned(g[j][part], c))
        for r in range(ROWS):
            for j in range(2):
                at = edge - sign * j
                for part in range(3):
                    out[part, r, at : at + 1, :] += sums[j][part][r : r + 1, :]
            at = edge - 2 * sign
            out[1, r, at : at + 1, :] += third[r : r + 1, :]


def build_bonds(words, bond, diag):
    def row(r, carry):
        lane = lax.broadcasted_iota(I32, (8, DEPTH), 1)
        for t in range(2):
            start = pl.multiple_of(r * COLS + 8 * t, 8)
            own = [words[w, r + 3, pl.ds(PAD + 8 * t, 8), :] for w in range(4)]
            totals = [None] * 6
            for c in range(-3, 4):
                if c:
                    outside = lane < c if c > 0 else lane >= DEPTH + c
                    near = [jnp.where(outside, I32(-1), pltpu.roll(own[w], c % DEPTH, 1)) for w in range(4)]
                else:
                    near = own
                sums = [None] * 6
                for b in range(-3, 4):
                    values = {}
                    for a in range(-3, 4):
                        k = NUMBER.get((a, b, c))
                        if k is None:
                            continue
                        word, bit = divmod(k, 31)
                        far_word, far_bit = divmod(BONDS - 1 - k, 31)
                        far = words[far_word, r + 3 + a, pl.ds(PAD + 8 * t + b, 8), :]
                        broken = (near[word] & I32(1 << bit)) | (far & I32(1 << far_bit))
                        value = jnp.where(broken == 0, F32(weight_of((a, b, c))), F32(0.0))
                        bond[k, pl.ds(start, 8), :] = value
                        if on_axis((a, b, c)):
                            at = 0 if a else (2 if b else 5)
                            sums[at] = add(sums[at], value)
                        else:
                            values[a] = value
                    if not values:
                        continue
                    zeroth, first = moments(values)
                    second = None
                    if 2 in values:
                        second = 4.0 * (values[2] + values[-2])
                    second = add(second, values[1] + values[-1])
                    sums[0] = add(sums[0], second)
                    if b:
                        sums[1] = plus_scaled(sums[1], b, first)
                        sums[2] = plus_scaled(sums[2], b * b, zeroth)
                    if c:
                        sums[3] = plus_scaled(sums[3], c, first)
                        sums[5] = plus_scaled(sums[5], c * c, zeroth)
                        if b:
                            sums[4] = plus_scaled(sums[4], b * c, zeroth)
                for n in range(6):
                    if sums[n] is not None:
                        totals[n] = add(totals[n], turned(sums[n], c))
            for n in range(6):
                diag[n, r, pl.ds(8 * t, 8), :] = totals[n]
        return carry

    lax.fori_loop(0, ROWS, row, 0)


def gather_edges(bond, bond_edge):
    for side in range(2):
        sign = 1 if side else -1
        edge = COLS - 1 if side else 0
        for n, (a, size, c, j, layer) in enumerate(EDGE):
            k = NUMBER[a, sign * size, c]
            bond_edge[side, n] = bond[k, pl.ds(edge - sign * j, ROWS, stride=COLS), :]


def kernel(
    nx, ny,
    disp, vel, load, flags, mask,
    u_out, v_out,
    field, near, far, rim, corner, rim_send, corner_send,
    words, words_rim, words_corner, words_rim_send, words_corner_send,
    bond, bond_edge, diag,
    force, state, keep, load_buf, flag_buf,
    ring_one, ring_two,
    in_sem, send_sem, recv_sem, word_send, word_recv, sum_send, sum_recv,
):
    rate, total, pull = state.at[0], state.at[1], keep.at[0]
    ax = lax.axis_index("gx")
    ay = lax.axis_index("gy")
    here = {-1: (ax > 0, ay > 0), 1: (ax < nx - 1, ay < ny - 1)}

    def exists(dx, dy):
        cond = None
        if dx:
            cond = here[dx][0]
        if dy:
            other = here[dy][1]
            cond = other if cond is None else cond & other
        return cond

    def device(dx, dy):
        return {"gx": ax + dx, "gy": ay + dy}

    sides = [(dx, dy) for dx in (-1, 0, 1) for dy in (-1, 0, 1) if dx or dy]
    diagonals = [(dx, dy) for dx, dy in sides if dx and dy]

    own_rows = pl.ds(3, ROWS)
    own_cols = pl.ds(PAD, COLS)
    loads = [
        pltpu.make_async_copy(disp, field.at[1, :, own_rows, own_cols], in_sem.at[0]),
        pltpu.make_async_copy(vel, field.at[0, :, own_rows, own_cols], in_sem.at[1]),
        pltpu.make_async_copy(mask, words.at[:, own_rows, own_cols], in_sem.at[2]),
        pltpu.make_async_copy(disp, u_out, in_sem.at[3]),
        pltpu.make_async_copy(vel, v_out, in_sem.at[4]),
        pltpu.make_async_copy(load, load_buf, in_sem.at[5]),
        pltpu.make_async_copy(flags, flag_buf, in_sem.at[6]),
    ]
    for copy in loads:
        copy.start()

    zero8 = jnp.zeros((8, DEPTH), F32)

    near[...] = jnp.zeros(near.shape, F32)
    far[...] = jnp.zeros(far.shape, F32)
    rim[...] = jnp.zeros(rim.shape, F32)
    words_rim[...] = jnp.full(words_rim.shape, -1, I32)
    words_corner[...] = jnp.full(words_corner.shape, -1, I32)
    for w in range(4):
        for r in list(range(3)) + list(range(TALL - 3, TALL)):
            words[w, r] = jnp.full((WIDE, DEPTH), -1, I32)

    barrier = pltpu.get_barrier_semaphore()
    for step in range(1, nx):
        pl.semaphore_signal(barrier, inc=1, device_id={"gx": lax.rem(ax + step, nx), "gy": ay})
    for step in range(1, ny):
        pl.semaphore_signal(barrier, inc=1, device_id={"gx": ax, "gy": lax.rem(ay + step, ny)})
    for dx, dy in diagonals:
        where = {"gx": lax.rem(ax + dx + nx, nx), "gy": lax.rem(ay + dy + ny, ny)}
        pl.semaphore_signal(barrier, inc=1, device_id=where)

    def clear(slot, carry):
        for part in range(3):
            for r in list(range(3)) + list(range(TALL - 3, TALL)):
                field[slot, part, r] = jnp.zeros((WIDE, DEPTH), F32)
            for r in range(3, TALL - 3):
                field[slot, part, r, 0:PAD, :] = zero8
                field[slot, part, r, PAD + COLS : WIDE, :] = zero8
        return carry

    lax.fori_loop(0, SLOTS, clear, 0)

    pl.semaphore_wait(barrier, nx + ny + 2)

    def edge_rows(dx):
        return (0, 2) if dx < 0 else (ROWS - 2, ROWS - 3)

    def halo_copies(slot, dx, dy):
        into = {-1: 1, 1: 0}
        if dx and dy:
            n = into[dx] * 2 + into[dy]
            return [(corner_send.at[slot, n], corner.at[slot, n], 6 + n)]
        if dx:
            first, third = edge_rows(dx)
            side = into[dx]
            return [
                (
                    field.at[slot, :, pl.ds(3 + first, 2), own_cols],
                    near.at[slot, side, :, :, own_cols],
                    side,
                ),
                (field.at[slot, 0, 3 + third, own_cols], far.at[slot, side, own_cols], 2 + side),
            ]
        side = into[dy]
        return [(rim_send.at[slot, side], rim.at[slot, side, :, pl.ds(8, 8)], 4 + side)]

    def halo_send(slot):
        for side in range(2):
            for part in range(3):
                for layer in range(3 if part == 1 else 2):
                    at = 6 if layer == 2 else part * 2 + layer
                    col = PAD + (layer if side else COLS - 1 - layer)
                    for r in range(ROWS):
                        rim_send[slot, side, at, r : r + 1, :] = field[slot, part, 3 + r, col : col + 1, :]
        for dx, dy in sides:
            if not (dx and dy):
                send_all(slot, dx, dy)
        for dx, dy in diagonals:
            n = (1 if dx < 0 else 0) * 2 + (1 if dy < 0 else 0)
            row = 3 + (0 if dx < 0 else ROWS - 2)
            col = PAD + (0 if dy < 0 else COLS - 2)
            for part in range(3):
                for e in range(2):
                    at = (part * 2 + e) * 2
                    corner_send[slot, n, at : at + 2, :] = field[slot, part, row + e, col : col + 2, :]
        for dx, dy in diagonals:
            send_all(slot, dx, dy)

    def send_all(slot, dx, dy):
        @pl.when(exists(dx, dy))
        def _():
            for src, dst, n in halo_copies(slot, dx, dy):
                pltpu.make_async_remote_copy(
                    src_ref=src, dst_ref=dst, send_sem=send_sem.at[slot, n], recv_sem=recv_sem.at[slot, n],
                    device_id=device(dx, dy),
                ).start()

    def halo_wait(slot):
        for dx, dy in sides:
            @pl.when(exists(dx, dy))
            def _():
                for src, dst, n in halo_copies(slot, dx, dy):
                    pltpu.make_async_remote_copy(
                        src_ref=src, dst_ref=dst, send_sem=send_sem.at[slot, n], recv_sem=recv_sem.at[slot, n],
                        device_id=device(dx, dy),
                    ).wait_send()
                for src, dst, n in halo_copies(slot, -dx, -dy):
                    pltpu.make_async_remote_copy(
                        src_ref=src, dst_ref=dst, send_sem=send_sem.at[slot, n], recv_sem=recv_sem.at[slot, n],
                        device_id=device(dx, dy),
                    ).wait_recv()
        for dx, dy in diagonals:
            sx, sy = (1 if dx > 0 else 0), (1 if dy > 0 else 0)
            at = PAD + COLS if sy else PAD - 2

            @pl.when(exists(dx, dy))
            def _():
                for part in range(3):
                    for e in range(2):
                        n = (part * 2 + e) * 2
                        near[slot, sx, part, e, at : at + 2, :] = corner[slot, sx * 2 + sy, n : n + 2, :]

    def word_copies(dx, dy):
        into = {-1: 1, 1: 0}
        if dx and dy:
            n = into[dx] * 2 + into[dy]
            return [(words_corner_send.at[n], words_corner.at[n], 4 + n)]
        if dx:
            first = 3 if dx < 0 else ROWS
            to = TALL - 3 if dx < 0 else 0
            return [(words.at[:, pl.ds(first, 3), own_cols], words.at[:, pl.ds(to, 3), own_cols], into[dx])]
        side = into[dy]
        return [(words_rim_send.at[side], words_rim.at[side], 2 + side)]

    def word_copy(dx, dy, src, dst, n):
        return pltpu.make_async_remote_copy(
            src_ref=src, dst_ref=dst, send_sem=word_send.at[n], recv_sem=word_recv.at[n], device_id=device(dx, dy),
        )

    for copy in (loads[0], loads[1]):
        copy.wait()
    halo_send(0)
    halo_send(1)
    loads[2].wait()
    for side in range(2):
        for w in range(4):
            for layer in range(3):
                col = PAD + (layer if side else COLS - 1 - layer)
                for r in range(ROWS):
                    words_rim_send[side, w, layer, r : r + 1, :] = words[w, 3 + r, col : col + 1, :]
    for dx, dy in diagonals:
        n = (1 if dx < 0 else 0) * 2 + (1 if dy < 0 else 0)
        row = 3 + (0 if dx < 0 else ROWS - 2)
        col = PAD + (0 if dy < 0 else COLS - 2)
        for w in range(4):
            for e in range(2):
                at = (w * 2 + e) * 2
                words_corner_send[n, at : at + 2, :] = words[w, row + e, col : col + 2, :]
    for dx, dy in sides:
        @pl.when(exists(dx, dy))
        def _():
            for src, dst, n in word_copies(dx, dy):
                word_copy(dx, dy, src, dst, n).start()
    for dx, dy in sides:
        @pl.when(exists(dx, dy))
        def _():
            for src, dst, n in word_copies(dx, dy):
                word_copy(dx, dy, src, dst, n).wait_send()
            for src, dst, n in word_copies(-dx, -dy):
                word_copy(dx, dy, src, dst, n).wait_recv()
    for side in range(2):
        for w in range(4):
            for layer in range(3):
                col = PAD + (COLS + layer if side else -1 - layer)
                for r in range(ROWS):
                    words[w, 3 + r, col : col + 1, :] = words_rim[side, w, layer, r : r + 1, :]
    for sx in range(2):
        for sy in range(2):
            row = 3 + (ROWS if sx else -2)
            col = PAD + (COLS if sy else -2)
            for w in range(4):
                for e in range(2):
                    at = (w * 2 + e) * 2
                    words[w, row + e, col : col + 2, :] = words_corner[sx * 2 + sy, at : at + 2, :]

    build_bonds(words, bond, diag)
    gather_edges(bond, bond_edge)

    def sum_copy(src, dst, which, turn, where):
        return pltpu.make_async_remote_copy(
            src_ref=src, dst_ref=dst, send_sem=sum_send.at[which, turn], recv_sem=sum_recv.at[which, turn],
            device_id=where,
        )

    def sum_begin(turn, rows):
        slab = jnp.concatenate([jnp.sum(row, axis=0, keepdims=True) for row in rows] + [jnp.zeros((2, DEPTH), F32)], axis=0)
        ring_one[turn, ax] = slab
        for step in range(1, nx):
            sum_copy(
                ring_one.at[turn, ax], ring_one.at[turn, ax], 0, turn, {"gx": lax.rem(ax + step, nx), "gy": ay}
            ).start()

    def sum_middle(turn):
        some = ring_one.at[turn, pl.ds(0, nx - 1)]
        copy = sum_copy(some, some, 0, turn, {"gx": ax, "gy": ay})
        copy.wait_recv()
        copy.wait_send()
        slab = ring_one[turn, 0]
        for n in range(1, nx):
            slab = slab + ring_one[turn, n]
        ring_two[turn, ay] = slab
        for step in range(1, ny):
            sum_copy(
                ring_two.at[turn, ay], ring_two.at[turn, ay], 1, turn, {"gx": ax, "gy": lax.rem(ay + step, ny)}
            ).start()

    def sum_end(turn):
        some = ring_two.at[turn, pl.ds(0, ny - 1)]
        copy = sum_copy(some, some, 1, turn, {"gx": ax, "gy": ay})
        copy.wait_recv()
        copy.wait_send()
        slab = ring_two[turn, 0]
        for n in range(1, ny):
            slab = slab + ring_two[turn, n]
        sums = jnp.broadcast_to(jnp.sum(slab, axis=1, keepdims=True), (8, DEPTH))
        return [jnp.broadcast_to(sums[n : n + 1, :], (8, DEPTH)) for n in range(6)]

    count = 3.0 * ROWS * nx * COLS * ny * DEPTH

    def damping_of(turn, alpha, beta):
        g0, g1, g2, h0, h1, h2 = sum_end(turn)
        kinetic = alpha * alpha * g0 + 2.0 * alpha * beta * g1 + beta * beta * g2
        rayleigh = -(alpha * alpha * h0 + alpha * beta * h1 + beta * beta * h2)
        rayleigh = jnp.maximum(rayleigh, 0.0)
        damping = 2.0 * jnp.sqrt((rayleigh / count) / (MASS * (kinetic / count + EPSILON)))
        return (2.0 - damping) / (2.0 + damping), 2.0 / (MASS * (2.0 + damping))

    def own(ref_slot, part, r, t):
        return field[ref_slot, part, 3 + r, pl.ds(PAD + 8 * t, 8), :]

    vregs = [(part, r, t) for part in range(3) for r in range(ROWS) for t in range(2)]

    def products(turn, slot, first):
        def body(r, carry):
            acc = list(carry)
            for part in range(3):
                for t in range(2):
                    at = (part, r, pl.ds(8 * t, 8), slice(None))
                    v, w = v_out[at], rate[at]
                    acc[0] += v * v
                    acc[3] += v * w
                    if not first:
                        tt, y = total[at], own(slot, part, r, t)
                        acc[1] += v * tt
                        acc[2] += tt * tt
                        acc[4] += v * y + tt * w
                        acc[5] += tt * y
            return tuple(acc)

        sum_begin(turn, lax.fori_loop(0, ROWS, body, (zero8,) * 6))

    def forces(slot):
        local_pass(slot, field, bond, diag, force)
        halo_wait(slot)
        across_pass(slot, near, far, bond, force)
        along_pass(slot, rim, bond_edge, force)

    for copy in loads[3:]:
        copy.wait()

    def first(n, carry):
        forces(n)
        loaded = n.astype(F32)

        def put(r, carry):
            for t in range(2):
                at = (r, pl.ds(8 * t, 8), slice(None))
                active = loaded * flag_buf[at].astype(F32)
                for part in range(3):
                    value = force[(part,) + at] + active * load_buf[(part,) + at]
                    state[(n, part) + at] = value
                    field[3 - n, part, 3 + r, pl.ds(PAD + 8 * t, 8), :] = value
            return carry

        lax.fori_loop(0, ROWS, put, 0)
        halo_send(3 - n)
        return carry

    lax.fori_loop(0, 2, first, 0)
    products(0, 0, True)

    def second(n, carry):
        forces(3 - n)

        def put(r, carry):
            for part in range(3):
                for t in range(2):
                    at = (part, r, pl.ds(8 * t, 8), slice(None))
                    value = force[at]
                    keep[(n,) + at] = value
                    field[0, part, 3 + r, pl.ds(PAD + 8 * t, 8), :] = value
            return carry

        lax.fori_loop(0, ROWS, put, 0)
        return carry

    lax.fori_loop(0, 2, second, 0)
    halo_send(0)
    sum_middle(0)
    products(1, 0, False)

    def advance(alpha, beta, slot):
        def body(r, carry):
            for part in range(3):
                for t in range(2):
                    at = (part, r, pl.ds(8 * t, 8), slice(None))
                    v, tt, w, y = v_out[at], total[at], rate[at], own(slot, part, r, t)
                    v = alpha * v + beta * tt
                    w = alpha * w + beta * y
                    v_out[at] = v
                    u_out[at] = u_out[at] + v
                    rate[at] = w
                    total[at] = tt + w
            return carry

        lax.fori_loop(0, ROWS, body, 0)

    def cycle(n, carry):
        alpha, beta = carry
        slot = lax.rem(n, 2)
        other = 1 - slot
        local_pass(slot, field, bond, diag, force)
        sum_middle(n + 1)
        halo_wait(slot)
        across_pass(slot, near, far, bond, force)
        along_pass(slot, rim, bond_edge, force)
        alpha, beta = damping_of(n, alpha, beta)

        def body(r, carry):
            for part in range(3):
                for t in range(2):
                    at = (part, r, pl.ds(8 * t, 8), slice(None))
                    x = alpha * pull[at] + beta * force[at]
                    pull[at] = x
                    field[other, part, 3 + r, pl.ds(PAD + 8 * t, 8), :] = own(slot, part, r, t) + x
            return carry

        lax.fori_loop(0, ROWS, body, 0)

        @pl.when(n < ITERS - 3)
        def _():
            halo_send(other)

        advance(alpha, beta, slot)
        products(n + 2, other, False)
        return alpha, beta

    one = jnp.ones((8, DEPTH), F32)
    alpha, beta = lax.fori_loop(0, ITERS - 2, cycle, (one, jnp.zeros((8, DEPTH), F32)))
    sum_middle(ITERS - 1)
    alpha, beta = damping_of(ITERS - 2, alpha, beta)
    advance(alpha, beta, (ITERS - 2) % 2)
    alpha, beta = damping_of(ITERS - 1, alpha, beta)

    def finish(r, carry):
        for part in range(3):
            for t in range(2):
                at = (part, r, pl.ds(8 * t, 8), slice(None))
                v = alpha * v_out[at] + beta * total[at]
                v_out[at] = v
                u_out[at] = u_out[at] + v
        return carry

    lax.fori_loop(0, ROWS, finish, 0)


def on_device(nx, ny, disp, vel, load, flags, mask_bits):
    block = (3, ROWS, COLS, DEPTH)
    any_spec = pl.BlockSpec(memory_space=pl.ANY)
    vmem_spec = pl.BlockSpec(memory_space=pltpu.VMEM)
    turns = ITERS
    dma = pltpu.SemaphoreType.DMA
    scratch = [
        pltpu.VMEM((SLOTS, 3, TALL, WIDE, DEPTH), F32),
        pltpu.VMEM((SLOTS, 2, 3, 2, WIDE, DEPTH), F32),
        pltpu.VMEM((SLOTS, 2, WIDE, DEPTH), F32),
        pltpu.VMEM((SLOTS, 2, 7, 24, DEPTH), F32),
        pltpu.VMEM((SLOTS, 4, 16, DEPTH), F32),
        pltpu.VMEM((SLOTS, 2, 7, 8, DEPTH), F32),
        pltpu.VMEM((SLOTS, 4, 16, DEPTH), F32),
        pltpu.VMEM((4, TALL, WIDE, DEPTH), I32),
        pltpu.VMEM((2, 4, 3, 8, DEPTH), I32),
        pltpu.VMEM((4, 16, DEPTH), I32),
        pltpu.VMEM((2, 4, 3, 8, DEPTH), I32),
        pltpu.VMEM((4, 16, DEPTH), I32),
        pltpu.VMEM((BONDS, ROWS * COLS, DEPTH), F32),
        pltpu.VMEM((2, len(EDGE), ROWS, DEPTH), F32),
        pltpu.VMEM((6, ROWS, COLS, DEPTH), F32),
        pltpu.VMEM(block, F32),
        pltpu.VMEM((2,) + block, F32),
        pltpu.VMEM((2,) + block, F32),
        pltpu.VMEM(block, F32),
        pltpu.VMEM(block[1:], I32),
        pltpu.VMEM((turns, nx, 8, DEPTH), F32),
        pltpu.VMEM((turns, ny, 8, DEPTH), F32),
        dma((7,)),
        dma((SLOTS, 10)),
        dma((SLOTS, 10)),
        dma((8,)),
        dma((8,)),
        dma((2, turns)),
        dma((2, turns)),
    ]
    return pl.pallas_call(
        functools.partial(kernel, nx, ny),
        out_shape=[jax.ShapeDtypeStruct(block, F32)] * 2,
        in_specs=[any_spec] * 5,
        out_specs=[vmem_spec] * 2,
        scratch_shapes=scratch,
        compiler_params=pltpu.CompilerParams(
            collective_id=0, has_side_effects=True, vmem_limit_bytes=40 * 1024 * 1024
        ),
    )(disp, vel, load, flags, mask_bits)


def solution(mesh):
    split = P(None, "gx", "gy", None)
    return jax.shard_map(
        functools.partial(on_device, mesh.shape["gx"], mesh.shape["gy"]),
        mesh=mesh,
        in_specs=(split, split, split, P("gx", "gy", None), split),
        out_specs=(split, split),
        check_vma=False,
    )
```

profile of v0, /device:TPU:0, one launch (start us, length us, event | category | flops | bytes accessed | tf_op | source)
XLA Modules:
  0.0 75.1 jit_solution(14382489089992466718)
XLA Ops:
  0.6 0.0 copy-start
  0.6 0.9 %copy-done = s32[4,8,16,128]{3,2,1,0:T(8,128)S(1)} copy-done((s32[4,8,16,128]{3,2,1,0:T(8,128)S(1)}, s32[4,8,16,128]{3,2,1,0:T(8,128)}, u32[]{:S(2)}) %copy-start) | copy-done | bytes 262168
  1.6 0.0 copy-start.1
  1.6 0.9 %copy-done.1 = f32[3,8,16,128]{3,2,1,0:T(8,128)S(1)} copy-done((f32[3,8,16,128]{3,2,1,0:T(8,128)S(1)}, f32[3,8,16,128]{3,2,1,0:T(8,128)}, u32[]{:S(2)}) %copy-start.1) | copy-done | bytes 196632
  2.5 0.0 copy-start.2
  2.5 0.9 %copy-done.2 = f32[3,8,16,128]{3,2,1,0:T(8,128)S(1)} copy-done((f32[3,8,16,128]{3,2,1,0:T(8,128)S(1)}, f32[3,8,16,128]{3,2,1,0:T(8,128)}, u32[]{:S(2)}) %copy-start.2) | copy-done | bytes 196632
  3.4 0.0 copy-start.3
  3.4 0.9 %copy-done.3 = f32[3,8,16,128]{3,2,1,0:T(8,128)S(1)} copy-done((f32[3,8,16,128]{3,2,1,0:T(8,128)S(1)}, f32[3,8,16,128]{3,2,1,0:T(8,128)}, u32[]{:S(2)}) %copy-start.3) | copy-done | bytes 196632
  4.4 0.0 copy-start.4
  4.4 0.8 %copy-done.4 = s32[8,16,128]{2,1,0:T(8,128)S(1)} copy-done((s32[8,16,128]{2,1,0:T(8,128)S(1)}, s32[8,16,128]{2,1,0:T(8,128)}, u32[]{:S(2)}) %copy-start.4) | copy-done | bytes 65560
  5.2 68.5 %shard_map.68 = (f32[3,8,16,128]{3,2,1,0:T(8,128)S(1)}, f32[3,8,16,128]{3,2,1,0:T(8,128)S(1)}) custom-call(f32[3,8,16,128]{3,2,1,0:T(8,128)S(1)} %copy-done.1, f32[3,8,16,128]{3,2,1,0:T(8,128)S(1)} %copy-done.2, f32[3,8,16,128]{3,2,1,0:T(8,128)S(1)} %copy-done.3, s32[8,16,128]{2,1,0:T(8,128)S(1)} %copy-done.4, s32[4,8,16,128]{3,2,1,0:T(8,128)S(1)} %copy-done), custom_call_target="tpu_custom_call" | custom-call | tf_op jit(solution)/shard_map/pallas_call | solution.py:866
  73.7 0.7 copy.9
  74.4 0.7 copy.10
Async XLA Ops:
  0.6 1.0 %copy-start = (s32[4,8,16,128]{3,2,1,0:T(8,128)S(1)}, s32[4,8,16,128]{3,2,1,0:T(8,128)}, u32[]{:S(2)}) copy-start(s32[4,8,16,128]{3,2,1,0:T(8,128)} %mask.1) | copy-start | bytes 786436
  1.6 0.9 %copy-start.1 = (f32[3,8,16,128]{3,2,1,0:T(8,128)S(1)}, f32[3,8,16,128]{3,2,1,0:T(8,128)}, u32[]{:S(2)}) copy-start(f32[3,8,16,128]{3,2,1,0:T(8,128)} %disp.1) | copy-start | bytes 589828
  2.5 0.9 %copy-start.2 = (f32[3,8,16,128]{3,2,1,0:T(8,128)S(1)}, f32[3,8,16,128]{3,2,1,0:T(8,128)}, u32[]{:S(2)}) copy-start(f32[3,8,16,128]{3,2,1,0:T(8,128)} %vel.1) | copy-start | bytes 589828
  3.4 0.9 %copy-start.3 = (f32[3,8,16,128]{3,2,1,0:T(8,128)S(1)}, f32[3,8,16,128]{3,2,1,0:T(8,128)}, u32[]{:S(2)}) copy-start(f32[3,8,16,128]{3,2,1,0:T(8,128)} %load.1) | copy-start | bytes 589828
  4.4 0.8 %copy-start.4 = (s32[8,16,128]{2,1,0:T(8,128)S(1)}, s32[8,16,128]{2,1,0:T(8,128)}, u32[]{:S(2)}) copy-start(s32[8,16,128]{2,1,0:T(8,128)} %flags.1) | copy-start | bytes 196612
where the time goes:
time: 75.8 us; the launch traced here: 75.1 us
  Pallas kernels  68.5 us (90%)
  local copies, waits for them, and re-layouts  5.92 us (8%)
    pallas_call x1, Pallas kernels, on_device(): pl.pallas_call(functools.partial(kernel, nx, ny), out_shape=[jax.ShapeDty...  68.5 us
    unnamed x12, local copies, waits for them, and re-layouts  5.92 us

commit v1 on v0

--- a/solution.py
+++ b/solution.py
@@ -95,6 +95,16 @@
         if factor and value is not None:
             out = plus_scaled(out, factor, value)
     return out
+
+
+def accumulate_first(total, factor, value):
+    if factor == 0 or value is None:
+        return total
+    if factor == 2:
+        return value
+    if factor == -2:
+        return 2.0 * (total - value)
+    return plus_scaled(total, factor, value)
 
 
 def turned(value, c):
@@ -186,18 +196,25 @@
                 for i in range(GROUP):
                     for part, value in enumerate((g0[i], g1[i], g2[i])):
                         if c == 0:
-                            u = [source(other, i, 0) for other in range(3)]
-                            own = None
-                            for other in range(3):
-                                pair = DIAG[min(part, other), max(part, other)]
-                                own = add(own, diag[pair, base + i, pl.ds(8 * t, 8), :] * u[other])
-                            value = -own if value is None else value - own
+                            if diag is not None:
+                                u = [source(other, i, 0) for other in range(3)]
+                                value = less_diagonal(value, diag, part, base + i, t, u)
+                            elif value is None:
+                                value = jnp.zeros((8, DEPTH), F32)
                             out[part, base + i, pl.ds(8 * t, 8), :] = value
                         elif value is not None:
                             out[part, base + i, pl.ds(8 * t, 8), :] += turned(value, c)
         return carry
 
     lax.fori_loop(0, ROWS // GROUP, group, 0)
+
+
+def less_diagonal(value, diag, part, r, t, u):
+    own = None
+    for other in range(3):
+        pair = DIAG[min(part, other), max(part, other)]
+        own = add(own, diag[pair, r, pl.ds(8 * t, 8), :] * u[other])
+    return -own if value is None else value - own
 
 
 DIAG = {(0, 0): 0, (0, 1): 1, (1, 1): 2, (0, 2): 3, (1, 2): 4, (2, 2): 5}
@@ -235,12 +252,12 @@
                     g[0][0] = g[0][0] + coef((3 * sign, 0, 0), 0) * far[slot, side, pl.ds(col, 8), :]
                 n0 = [None] * 2
                 n1 = [None] * 2
+                deep = [None] * 2
                 for b in (2, -2, 1, -1, 0):
                     reach = oblique(b, c)
                     if not reach:
                         continue
                     zeroth = [None] * 2
-                    deep = [None] * 2
                     for layer in range(max(reach)):
                         u0 = source(0, layer, b)
                         u1 = source(1, layer, b) if b else None
@@ -249,23 +266,27 @@
                         for i in range(2):
                             size = i + layer + 1
                             a = sign * size
-                            if a in reach:
+                            if a not in reach:
+                                continue
+                            if size == 2 and i == 1:
+                                q = plus_scaled(q, sign, u0)
+                            else:
                                 q = plus_scaled(s, a, u0)
-                                term = coef((a, b, c), i) * q
-                                zeroth[i] = add(zeroth[i], term)
-                                if size == 1:
-                                    g[i][0] = plus_scaled(g[i][0], sign, term)
-                                else:
-                                    deep[i] = add(deep[i], term)
+                            term = coef((a, b, c), i) * q
+                            zeroth[i] = add(zeroth[i], term)
+                            if size == 1:
+                                g[i][0] = plus_scaled(g[i][0], sign, term)
+                            else:
+                                deep[i] = add(deep[i], term)
                     for i in range(2):
-                        if deep[i] is not None:
-                            g[i][0] = plus_scaled(g[i][0], 2 * sign, deep[i])
                         if zeroth[i] is None:
                             continue
                         if c:
                             n0[i] = add(n0[i], zeroth[i])
-                        if b:
-                            n1[i] = plus_scaled(n1[i], b, zeroth[i])
+                        n1[i] = accumulate_first(n1[i], b, zeroth[i])
+                for i in range(2):
+                    if deep[i] is not None:
+                        g[i][0] = plus_scaled(g[i][0], 2 * sign, deep[i])
                 for i in range(2):
                     g[i][1] = n1[i]
                     g[i][2] = scaled(c, n0[i]) if c else None
@@ -279,10 +300,10 @@
             out[0, edge - 2 * sign, pl.ds(8 * t, 8), :] += third
 
 
-def along_pass(slot, rim, bond_edge, out):
+def along_terms(slot, rim, bond_edge):
+    found = []
     for side in range(2):
         sign = 1 if side else -1
-        edge = COLS - 1 if side else 0
 
         def coef(a, size, c, j):
             return bond_edge[side, EDGE_AT[a, size, c, j]]
@@ -306,12 +327,12 @@
                             third = term
             n0 = [None] * 2
             n1 = [None] * 2
+            deep = [None] * 2
             for a in (2, -2, 1, -1, 0):
                 reach = [size for size in (1, 2) if (a, size, c) in NUMBER and not on_axis((a, size, c))]
                 if not reach:
                     continue
                 zeroth = [None] * 2
-                deep = [None] * 2
                 for layer in range(max(reach)):
                     u0 = source(0, layer, a) if a else None
                     u1 = source(1, layer, a)
@@ -319,50 +340,80 @@
                     s = combine((a, c), (u0, u2))
                     for j in range(2):
                         size = j + layer + 1
-                        if size in reach:
-                            term = coef(a, size, c, j) * plus_scaled(s, sign * size, u1)
-                            zeroth[j] = add(zeroth[j], term)
-                            if size == 1:
-                                g[j][1] = plus_scaled(g[j][1], sign, term)
-                            else:
-                                deep[j] = add(deep[j], term)
+                        if size not in reach:
+                            continue
+                        if size == 2 and j == 1:
+                            q = plus_scaled(q, sign, u1)
+                        else:
+                            q = plus_scaled(s, sign * size, u1)
+                        term = coef(a, size, c, j) * q
+                        zeroth[j] = add(zeroth[j], term)
+                        if size == 1:
+                            g[j][1] = plus_scaled(g[j][1], sign, term)
+                        else:
+                            deep[j] = add(deep[j], term)
                 for j in range(2):
-                    if deep[j] is not None:
-                        g[j][1] = plus_scaled(g[j][1], 2 * sign, deep[j])
                     if zeroth[j] is None:
                         continue
                     if c:
                         n0[j] = add(n0[j], zeroth[j])
-                    if a:
-                        n1[j] = plus_scaled(n1[j], a, zeroth[j])
+                    n1[j] = accumulate_first(n1[j], a, zeroth[j])
+            for j in range(2):
+                if deep[j] is not None:
+                    g[j][1] = plus_scaled(g[j][1], 2 * sign, deep[j])
             for j in range(2):
                 g[j][0] = n1[j]
                 g[j][2] = scaled(c, n0[j]) if c else None
                 for part in range(3):
                     if g[j][part] is not None:
                         sums[j][part] = add(sums[j][part], turned(g[j][part], c))
-        for r in range(ROWS):
-            for j in range(2):
-                at = edge - sign * j
-                for part in range(3):
-                    out[part, r, at : at + 1, :] += sums[j][part][r : r + 1, :]
-            at = edge - 2 * sign
-            out[1, r, at : at + 1, :] += third[r : r + 1, :]
+        found.append([(part, j, sums[j][part]) for part in range(3) for j in range(2)] + [(1, 2, third)])
+    return found
+
+
+def spread(found, put):
+    for side in range(2):
+        for part, j, value in found[side]:
+            at = COLS - 1 - j if side else j
+            for r in range(ROWS):
+                put(part, r, at, value[r : r + 1, :])
+
+
+def weight_if_intact(near, far, offset):
+    k = NUMBER[offset]
+    word, bit = divmod(k, 31)
+    far_word, far_bit = divmod(BONDS - 1 - k, 31)
+    broken = (near[word] & I32(1 << bit)) | (far(far_word) & I32(1 << far_bit))
+    return jnp.where(broken == 0, F32(weight_of(offset)), F32(0.0))
+
+
+def moved(own, c):
+    if not c:
+        return own
+    lane = lax.broadcasted_iota(I32, (8, DEPTH), 1)
+    outside = lane < c if c > 0 else lane >= DEPTH + c
+    return [jnp.where(outside, I32(-1), pltpu.roll(word, c % DEPTH, 1)) for word in own]
+
+
+def tally(sums, offset, value):
+    a, b, c = offset
+    if on_axis(offset):
+        at = 0 if a else (2 if b else 5)
+        sums[at] = add(sums[at], value)
+        return
+    for at, factor in enumerate((a * a, a * b, b * b, a * c, b * c, c * c)):
+        if factor:
+            sums[at] = plus_scaled(sums[at], factor, value)
 
 
 def build_bonds(words, bond, diag):
     def row(r, carry):
-        lane = lax.broadcasted_iota(I32, (8, DEPTH), 1)
         for t in range(2):
             start = pl.multiple_of(r * COLS + 8 * t, 8)
             own = [words[w, r + 3, pl.ds(PAD + 8 * t, 8), :] for w in range(4)]
             totals = [None] * 6
             for c in range(-3, 4):
-                if c:
-                    outside = lane < c if c > 0 else lane >= DEPTH + c
-                    near = [jnp.where(outside, I32(-1), pltpu.roll(own[w], c % DEPTH, 1)) for w in range(4)]
-                else:
-                    near = own
+                near = moved(own, c)
                 sums = [None] * 6
                 for b in range(-3, 4):
                     values = {}
@@ -370,15 +421,14 @@
                         k = NUMBER.get((a, b, c))
                         if k is None:
                             continue
-                        word, bit = divmod(k, 31)
-                        far_word, far_bit = divmod(BONDS - 1 - k, 31)
-                        far = words[far_word, r + 3 + a, pl.ds(PAD + 8 * t + b, 8), :]
-                        broken = (near[word] & I32(1 << bit)) | (far & I32(1 << far_bit))
-                        value = jnp.where(broken == 0, F32(weight_of((a, b, c))), F32(0.0))
+
+                        def far(w):
+                            return words[w, r + 3 + a, pl.ds(PAD + 8 * t + b, 8), :]
+
+                        value = weight_if_intact(near, far, (a, b, c))
                         bond[k, pl.ds(start, 8), :] = value
                         if on_axis((a, b, c)):
-                            at = 0 if a else (2 if b else 5)
-                            sums[at] = add(sums[at], value)
+                            tally(sums, (a, b, c), value)
                         else:
                             values[a] = value
                     if not values:
@@ -407,13 +457,72 @@
     lax.fori_loop(0, ROWS, row, 0)
 
 
-def gather_edges(bond, bond_edge):
+def build_across(words, words_near, bond, diag):
+    for side in range(2):
+        sign = 1 if side else -1
+        edge = ROWS - 1 if side else 0
+        for t in range(2):
+            for i in range(3):
+                r = edge - sign * i
+                own = [words[w, r + 3, pl.ds(PAD + 8 * t, 8), :] for w in range(4)]
+                totals = [None] * 6
+                for c in range(-2, 3):
+                    if i == 2 and c:
+                        continue
+                    near = moved(own, c)
+                    sums = [None] * 6
+                    for b in range(-2, 3):
+                        for layer in range(3 - i):
+                            offset = (sign * (i + layer + 1), b, c)
+                            if offset not in NUMBER:
+                                continue
+
+                            def far(w):
+                                e = layer if side else 2 - layer
+                                return words_near[side, w, e, pl.ds(PAD + 8 * t + b, 8), :]
+
+                            value = weight_if_intact(near, far, offset)
+                            bond[NUMBER[offset], pl.ds(r * COLS + 8 * t, 8), :] = value
+                            tally(sums, offset, value)
+                    for n in range(6):
+                        if sums[n] is not None:
+                            totals[n] = add(totals[n], turned(sums[n], c))
+                for n in range(6):
+                    if totals[n] is not None:
+                        diag[n, r, pl.ds(8 * t, 8), :] += totals[n]
+
+
+def build_along(words_mine, words_rim, bond_edge, diag):
     for side in range(2):
         sign = 1 if side else -1
         edge = COLS - 1 if side else 0
-        for n, (a, size, c, j, layer) in enumerate(EDGE):
-            k = NUMBER[a, sign * size, c]
-            bond_edge[side, n] = bond[k, pl.ds(edge - sign * j, ROWS, stride=COLS), :]
+        for j in range(3):
+            own = [words_mine[1 - side, w, j] for w in range(4)]
+            totals = [None] * 6
+            for c in range(-2, 3):
+                if j == 2 and c:
+                    continue
+                near = moved(own, c)
+                sums = [None] * 6
+                for n, (a, size, up, col, layer) in enumerate(EDGE):
+                    if col != j or up != c:
+                        continue
+                    offset = (a, sign * size, c)
+
+                    def far(w):
+                        return words_rim[side, w, layer, pl.ds(8 + a, 8), :]
+
+                    value = weight_if_intact(near, far, offset)
+                    bond_edge[side, n] = value
+                    tally(sums, offset, value)
+                for n in range(6):
+                    if sums[n] is not None:
+                        totals[n] = add(totals[n], turned(sums[n], c))
+            at = edge - sign * j
+            for n in range(6):
+                if totals[n] is not None:
+                    for r in range(ROWS):
+                        diag[n, r, at : at + 1, :] += totals[n][r : r + 1, :]
 
 
 def kernel(
@@ -421,13 +530,13 @@
     disp, vel, load, flags, mask,
     u_out, v_out,
     field, near, far, rim, corner, rim_send, corner_send,
-    words, words_rim, words_corner, words_rim_send, words_corner_send,
+    words, words_near, words_rim, words_corner, words_rim_send, words_corner_send,
     bond, bond_edge, diag,
-    force, state, keep, load_buf, flag_buf,
+    pool, load_buf, flag_buf,
     ring_one, ring_two,
     in_sem, send_sem, recv_sem, word_send, word_recv, sum_send, sum_recv,
 ):
-    rate, total, pull = state.at[0], state.at[1], keep.at[0]
+    total, rate, force, pull = (pool.at[n] for n in range(4))
     ax = lax.axis_index("gx")
     ay = lax.axis_index("gy")
     here = {-1: (ax > 0, ay > 0), 1: (ax < nx - 1, ay < ny - 1)}
@@ -450,9 +559,9 @@
     own_rows = pl.ds(3, ROWS)
     own_cols = pl.ds(PAD, COLS)
     loads = [
-        pltpu.make_async_copy(disp, field.at[1, :, own_rows, own_cols], in_sem.at[0]),
-        pltpu.make_async_copy(vel, field.at[0, :, own_rows, own_cols], in_sem.at[1]),
-        pltpu.make_async_copy(mask, words.at[:, own_rows, own_cols], in_sem.at[2]),
+        pltpu.make_async_copy(mask, words.at[:, own_rows, own_cols], in_sem.at[0]),
+        pltpu.make_async_copy(vel, field.at[1, :, own_rows, own_cols], in_sem.at[1]),
+        pltpu.make_async_copy(disp, field.at[0, :, own_rows, own_cols], in_sem.at[2]),
         pltpu.make_async_copy(disp, u_out, in_sem.at[3]),
         pltpu.make_async_copy(vel, v_out, in_sem.at[4]),
         pltpu.make_async_copy(load, load_buf, in_sem.at[5]),
@@ -462,15 +571,6 @@
         copy.start()
 
     zero8 = jnp.zeros((8, DEPTH), F32)
-
-    near[...] = jnp.zeros(near.shape, F32)
-    far[...] = jnp.zeros(far.shape, F32)
-    rim[...] = jnp.zeros(rim.shape, F32)
-    words_rim[...] = jnp.full(words_rim.shape, -1, I32)
-    words_corner[...] = jnp.full(words_corner.shape, -1, I32)
-    for w in range(4):
-        for r in list(range(3)) + list(range(TALL - 3, TALL)):
-            words[w, r] = jnp.full((WIDE, DEPTH), -1, I32)
 
     barrier = pltpu.get_barrier_semaphore()
     for step in range(1, nx):
@@ -481,18 +581,66 @@
         where = {"gx": lax.rem(ax + dx + nx, nx), "gy": lax.rem(ay + dy + ny, ny)}
         pl.semaphore_signal(barrier, inc=1, device_id=where)
 
-    def clear(slot, carry):
-        for part in range(3):
-            for r in list(range(3)) + list(range(TALL - 3, TALL)):
-                field[slot, part, r] = jnp.zeros((WIDE, DEPTH), F32)
-            for r in range(3, TALL - 3):
-                field[slot, part, r, 0:PAD, :] = zero8
-                field[slot, part, r, PAD + COLS : WIDE, :] = zero8
-        return carry
-
-    lax.fori_loop(0, SLOTS, clear, 0)
-
-    pl.semaphore_wait(barrier, nx + ny + 2)
+
+    inner = slice(PAD, PAD + COLS)
+    pads = (slice(0, PAD), slice(PAD + COLS, WIDE))
+    borders = list(range(3)) + list(range(TALL - 3, TALL))
+
+    def broken(*shape):
+        return jnp.full(shape + (DEPTH,), -1, I32)
+
+    def clear():
+        def slot_clear(slot, carry):
+            for part in range(3):
+                for r in borders:
+                    field[slot, part, r] = jnp.zeros((WIDE, DEPTH), F32)
+                for r in range(3, TALL - 3):
+                    for pad in pads:
+                        field[slot, part, r, pad, :] = zero8
+                for side in range(2):
+                    for e in range(2):
+                        for pad in pads:
+                            near[slot, side, part, e, pad, :] = zero8
+            for side in range(2):
+                for at in range(7):
+                    rim[slot, side, at, 0:8, :] = zero8
+                    rim[slot, side, at, 16:24, :] = zero8
+            return carry
+
+        lax.fori_loop(0, SLOTS, slot_clear, 0)
+        for w in range(4):
+            for r in range(TALL):
+                if r in borders:
+                    words[w, r] = broken(WIDE)
+                else:
+                    for pad in pads:
+                        words[w, r, pad, :] = broken(PAD)
+            for side in range(2):
+                for layer in range(3):
+                    for pad in pads:
+                        words_near[side, w, layer, pad, :] = broken(PAD)
+                    words_rim[side, w, layer, 0:8, :] = broken(8)
+                    words_rim[side, w, layer, 16:24, :] = broken(8)
+        for side in range(2):
+            @pl.when(ax == (nx - 1 if side else 0))
+            def _():
+                for slot in range(SLOTS):
+                    far[slot, side, inner, :] = jnp.zeros((COLS, DEPTH), F32)
+                    for part in range(3):
+                        for e in range(2):
+                            near[slot, side, part, e, inner, :] = jnp.zeros((COLS, DEPTH), F32)
+                for w in range(4):
+                    for layer in range(3):
+                        words_near[side, w, layer, inner, :] = broken(COLS)
+
+            @pl.when(ay == (ny - 1 if side else 0))
+            def _():
+                for slot in range(SLOTS):
+                    for at in range(7):
+                        rim[slot, side, at, 8:16, :] = zero8
+                for w in range(4):
+                    for layer in range(3):
+                        words_rim[side, w, layer, 8:16, :] = broken(8)
 
     def edge_rows(dx):
         return (0, 2) if dx < 0 else (ROWS - 2, ROWS - 3)
@@ -516,61 +664,72 @@
         side = into[dy]
         return [(rim_send.at[slot, side], rim.at[slot, side, :, pl.ds(8, 8)], 4 + side)]
 
-    def halo_send(slot):
+    def spot(part, layer):
+        return 6 if layer == 2 else part * 2 + layer
+
+    def pack_rim(slot):
         for side in range(2):
             for part in range(3):
                 for layer in range(3 if part == 1 else 2):
-                    at = 6 if layer == 2 else part * 2 + layer
                     col = PAD + (layer if side else COLS - 1 - layer)
                     for r in range(ROWS):
-                        rim_send[slot, side, at, r : r + 1, :] = field[slot, part, 3 + r, col : col + 1, :]
-        for dx, dy in sides:
-            if not (dx and dy):
-                send_all(slot, dx, dy)
-        for dx, dy in diagonals:
-            n = (1 if dx < 0 else 0) * 2 + (1 if dy < 0 else 0)
-            row = 3 + (0 if dx < 0 else ROWS - 2)
-            col = PAD + (0 if dy < 0 else COLS - 2)
-            for part in range(3):
-                for e in range(2):
-                    at = (part * 2 + e) * 2
-                    corner_send[slot, n, at : at + 2, :] = field[slot, part, row + e, col : col + 2, :]
-        for dx, dy in diagonals:
-            send_all(slot, dx, dy)
-
-    def send_all(slot, dx, dy):
-        @pl.when(exists(dx, dy))
-        def _():
-            for src, dst, n in halo_copies(slot, dx, dy):
-                pltpu.make_async_remote_copy(
-                    src_ref=src, dst_ref=dst, send_sem=send_sem.at[slot, n], recv_sem=recv_sem.at[slot, n],
-                    device_id=device(dx, dy),
-                ).start()
-
-    def halo_wait(slot):
-        for dx, dy in sides:
+                        rim_send[slot, side, spot(part, layer), r : r + 1, :] = field[
+                            slot, part, 3 + r, col : col + 1, :
+                        ]
+
+    def ends(dx):
+        return slice(0, 2) if dx < 0 else slice(ROWS - 2, ROWS)
+
+    def beyond(dx):
+        return slice(6, 8) if dx < 0 else slice(16, 18)
+
+    def copy_of(slot, dx, dy, src, dst, n):
+        return pltpu.make_async_remote_copy(
+            src_ref=src, dst_ref=dst, send_sem=send_sem.at[slot, n], recv_sem=recv_sem.at[slot, n],
+            device_id=device(dx, dy),
+        )
+
+    along = [(0, -1), (0, 1)]
+    across = [(-1, 0), (1, 0)]
+
+    def send_all(slot, which):
+        for dx, dy in which:
             @pl.when(exists(dx, dy))
             def _():
                 for src, dst, n in halo_copies(slot, dx, dy):
-                    pltpu.make_async_remote_copy(
-                        src_ref=src, dst_ref=dst, send_sem=send_sem.at[slot, n], recv_sem=recv_sem.at[slot, n],
-                        device_id=device(dx, dy),
-                    ).wait_send()
+                    copy_of(slot, dx, dy, src, dst, n).start()
+
+    def send_rim(slot):
+        send_all(slot, along)
+        for dx, dy in diagonals:
+            n = (1 if dx < 0 else 0) * 2 + (1 if dy < 0 else 0)
+            for at in range(6):
+                corner_send[slot, n, 2 * at : 2 * at + 2, :] = rim_send[slot, 1 if dy < 0 else 0, at, ends(dx), :]
+        send_all(slot, diagonals)
+
+    def halo_send(slot):
+        pack_rim(slot)
+        send_rim(slot)
+        send_all(slot, across)
+
+    def wait_all(slot, which):
+        for dx, dy in which:
+            @pl.when(exists(dx, dy))
+            def _():
+                for src, dst, n in halo_copies(slot, dx, dy):
+                    copy_of(slot, dx, dy, src, dst, n).wait_send()
                 for src, dst, n in halo_copies(slot, -dx, -dy):
-                    pltpu.make_async_remote_copy(
-                        src_ref=src, dst_ref=dst, send_sem=send_sem.at[slot, n], recv_sem=recv_sem.at[slot, n],
-                        device_id=device(dx, dy),
-                    ).wait_recv()
+                    copy_of(slot, dx, dy, src, dst, n).wait_recv()
+
+    def wait_rim(slot):
+        wait_all(slot, along + diagonals)
         for dx, dy in diagonals:
             sx, sy = (1 if dx > 0 else 0), (1 if dy > 0 else 0)
-            at = PAD + COLS if sy else PAD - 2
 
             @pl.when(exists(dx, dy))
             def _():
-                for part in range(3):
-                    for e in range(2):
-                        n = (part * 2 + e) * 2
-                        near[slot, sx, part, e, at : at + 2, :] = corner[slot, sx * 2 + sy, n : n + 2, :]
+                for at in range(6):
+                    rim[slot, sy, at, beyond(dx), :] = corner[slot, sx * 2 + sy, 2 * at : 2 * at + 2, :]
 
     def word_copies(dx, dy):
         into = {-1: 1, 1: 0}
@@ -579,21 +738,16 @@
             return [(words_corner_send.at[n], words_corner.at[n], 4 + n)]
         if dx:
             first = 3 if dx < 0 else ROWS
-            to = TALL - 3 if dx < 0 else 0
-            return [(words.at[:, pl.ds(first, 3), own_cols], words.at[:, pl.ds(to, 3), own_cols], into[dx])]
+            return [(words.at[:, pl.ds(first, 3), own_cols], words_near.at[into[dx], :, :, own_cols], into[dx])]
         side = into[dy]
-        return [(words_rim_send.at[side], words_rim.at[side], 2 + side)]
+        return [(words_rim_send.at[side], words_rim.at[side, :, :, pl.ds(8, 8)], 2 + side)]
 
     def word_copy(dx, dy, src, dst, n):
         return pltpu.make_async_remote_copy(
             src_ref=src, dst_ref=dst, send_sem=word_send.at[n], recv_sem=word_recv.at[n], device_id=device(dx, dy),
         )
 
-    for copy in (loads[0], loads[1]):
-        copy.wait()
-    halo_send(0)
-    halo_send(1)
-    loads[2].wait()
+    loads[0].wait()
     for side in range(2):
         for w in range(4):
             for layer in range(3):
@@ -602,41 +756,42 @@
                     words_rim_send[side, w, layer, r : r + 1, :] = words[w, 3 + r, col : col + 1, :]
     for dx, dy in diagonals:
         n = (1 if dx < 0 else 0) * 2 + (1 if dy < 0 else 0)
-        row = 3 + (0 if dx < 0 else ROWS - 2)
-        col = PAD + (0 if dy < 0 else COLS - 2)
         for w in range(4):
-            for e in range(2):
-                at = (w * 2 + e) * 2
-                words_corner_send[n, at : at + 2, :] = words[w, row + e, col : col + 2, :]
+            for layer in range(2):
+                at = (w * 2 + layer) * 2
+                words_corner_send[n, at : at + 2, :] = words_rim_send[1 if dy < 0 else 0, w, layer, ends(dx), :]
+    pl.semaphore_wait(barrier, nx + ny + 2)
     for dx, dy in sides:
         @pl.when(exists(dx, dy))
         def _():
             for src, dst, n in word_copies(dx, dy):
                 word_copy(dx, dy, src, dst, n).start()
-    for dx, dy in sides:
-        @pl.when(exists(dx, dy))
-        def _():
-            for src, dst, n in word_copies(dx, dy):
-                word_copy(dx, dy, src, dst, n).wait_send()
-            for src, dst, n in word_copies(-dx, -dy):
-                word_copy(dx, dy, src, dst, n).wait_recv()
-    for side in range(2):
-        for w in range(4):
-            for layer in range(3):
-                col = PAD + (COLS + layer if side else -1 - layer)
-                for r in range(ROWS):
-                    words[w, 3 + r, col : col + 1, :] = words_rim[side, w, layer, r : r + 1, :]
-    for sx in range(2):
-        for sy in range(2):
-            row = 3 + (ROWS if sx else -2)
-            col = PAD + (COLS if sy else -2)
-            for w in range(4):
-                for e in range(2):
-                    at = (w * 2 + e) * 2
-                    words[w, row + e, col : col + 2, :] = words_corner[sx * 2 + sy, at : at + 2, :]
-
+    for n in range(2):
+        loads[2 - n].wait()
+        halo_send(n)
+
+    clear()
     build_bonds(words, bond, diag)
-    gather_edges(bond, bond_edge)
+    def words_wait():
+        for dx, dy in sides:
+            @pl.when(exists(dx, dy))
+            def _():
+                for src, dst, n in word_copies(dx, dy):
+                    word_copy(dx, dy, src, dst, n).wait_send()
+                for src, dst, n in word_copies(-dx, -dy):
+                    word_copy(dx, dy, src, dst, n).wait_recv()
+        for dx, dy in diagonals:
+            sx, sy = (1 if dx > 0 else 0), (1 if dy > 0 else 0)
+
+            @pl.when(exists(dx, dy))
+            def _():
+                for w in range(4):
+                    for layer in range(2):
+                        at = (w * 2 + layer) * 2
+                        words_rim[sy, w, layer, beyond(dx), :] = words_corner[sx * 2 + sy, at : at + 2, :]
+
+        build_across(words, words_near, bond, diag)
+        build_along(words_rim_send, words_rim, bond_edge, diag)
 
     def sum_copy(src, dst, which, turn, where):
         return pltpu.make_async_remote_copy(
@@ -646,7 +801,9 @@
 
     def sum_begin(turn, rows):
         slab = jnp.concatenate([jnp.sum(row, axis=0, keepdims=True) for row in rows] + [jnp.zeros((2, DEPTH), F32)], axis=0)
-        ring_one[turn, ax] = slab
+        each = jnp.broadcast_to(jnp.sum(slab, axis=1, keepdims=True), (8, DEPTH))
+        mine = lax.broadcasted_iota(I32, (8, DEPTH), 0) == lax.broadcasted_iota(I32, (8, DEPTH), 1)
+        ring_one[turn, ax] = jnp.sum(jnp.where(mine, each, 0.0), axis=0, keepdims=True)
         for step in range(1, nx):
             sum_copy(
                 ring_one.at[turn, ax], ring_one.at[turn, ax], 0, turn, {"gx": lax.rem(ax + step, nx), "gy": ay}
@@ -657,10 +814,7 @@
         copy = sum_copy(some, some, 0, turn, {"gx": ax, "gy": ay})
         copy.wait_recv()
         copy.wait_send()
-        slab = ring_one[turn, 0]
-        for n in range(1, nx):
-            slab = slab + ring_one[turn, n]
-        ring_two[turn, ay] = slab
+        ring_two[turn, ay] = jnp.sum(ring_one[turn], axis=0)
         for step in range(1, ny):
             sum_copy(
                 ring_two.at[turn, ay], ring_two.at[turn, ay], 1, turn, {"gx": ax, "gy": lax.rem(ay + step, ny)}
@@ -671,11 +825,8 @@
         copy = sum_copy(some, some, 1, turn, {"gx": ax, "gy": ay})
         copy.wait_recv()
         copy.wait_send()
-        slab = ring_two[turn, 0]
-        for n in range(1, ny):
-            slab = slab + ring_two[turn, n]
-        sums = jnp.broadcast_to(jnp.sum(slab, axis=1, keepdims=True), (8, DEPTH))
-        return [jnp.broadcast_to(sums[n : n + 1, :], (8, DEPTH)) for n in range(6)]
+        row = jnp.sum(ring_two[turn], axis=0)
+        return [jnp.broadcast_to(row[:, n : n + 1], (8, DEPTH)) for n in range(6)]
 
     count = 3.0 * ROWS * nx * COLS * ny * DEPTH
 
@@ -711,55 +862,61 @@
 
         sum_begin(turn, lax.fori_loop(0, ROWS, body, (zero8,) * 6))
 
-    def forces(slot):
-        local_pass(slot, field, bond, diag, force)
-        halo_wait(slot)
-        across_pass(slot, near, far, bond, force)
-        along_pass(slot, rim, bond_edge, force)
+    def rest(slot, out):
+        wait_all(slot, across)
+        across_pass(slot, near, far, bond, out)
+        wait_rim(slot)
+
+        def put(part, r, at, value):
+            out[part, r, at : at + 1, :] += value
+
+        spread(along_terms(slot, rim, bond_edge), put)
 
     for copy in loads[3:]:
         copy.wait()
 
-    def first(n, carry):
-        forces(n)
-        loaded = n.astype(F32)
+    def begin(n, carry):
+        out = pool.at[n]
+        local_pass(n, field, bond, None, out)
+
+        @pl.when(n == 0)
+        def _():
+            words_wait()
+
+        rest(n, out)
+        loaded = lax.div(3 - n, 3).astype(F32)
+        to = lax.rem(n + 2, 4)
 
         def put(r, carry):
             for t in range(2):
                 at = (r, pl.ds(8 * t, 8), slice(None))
                 active = loaded * flag_buf[at].astype(F32)
+                u = [own(n, part, r, t) for part in range(3)]
                 for part in range(3):
-                    value = force[(part,) + at] + active * load_buf[(part,) + at]
-                    state[(n, part) + at] = value
-                    field[3 - n, part, 3 + r, pl.ds(PAD + 8 * t, 8), :] = value
+                    value = less_diagonal(out[(part,) + at], diag, part, r, t, u)
+                    value = value + active * load_buf[(part,) + at]
+                    out[(part,) + at] = value
+                    field[to, part, 3 + r, pl.ds(PAD + 8 * t, 8), :] = value
             return carry
 
         lax.fori_loop(0, ROWS, put, 0)
-        halo_send(3 - n)
+
+        @pl.when(n < 3)
+        def _():
+            halo_send(to)
+
+        @pl.when(n == 1)
+        def _():
+            products(0, 0, True)
+
+        @pl.when(n == 2)
+        def _():
+            sum_middle(0)
+            products(1, 0, False)
+
         return carry
 
-    lax.fori_loop(0, 2, first, 0)
-    products(0, 0, True)
-
-    def second(n, carry):
-        forces(3 - n)
-
-        def put(r, carry):
-            for part in range(3):
-                for t in range(2):
-                    at = (part, r, pl.ds(8 * t, 8), slice(None))
-                    value = force[at]
-                    keep[(n,) + at] = value
-                    field[0, part, 3 + r, pl.ds(PAD + 8 * t, 8), :] = value
-            return carry
-
-        lax.fori_loop(0, ROWS, put, 0)
-        return carry
-
-    lax.fori_loop(0, 2, second, 0)
-    halo_send(0)
-    sum_middle(0)
-    products(1, 0, False)
+    lax.fori_loop(0, 4, begin, 0)
 
     def advance(alpha, beta, slot):
         def body(r, carry):
@@ -782,10 +939,9 @@
         slot = lax.rem(n, 2)
         other = 1 - slot
         local_pass(slot, field, bond, diag, force)
+        wait_all(slot, across)
+        across_pass(slot, near, far, bond, force)
         sum_middle(n + 1)
-        halo_wait(slot)
-        across_pass(slot, near, far, bond, force)
-        along_pass(slot, rim, bond_edge, force)
         alpha, beta = damping_of(n, alpha, beta)
 
         def body(r, carry):
@@ -798,10 +954,27 @@
             return carry
 
         lax.fori_loop(0, ROWS, body, 0)
-
-        @pl.when(n < ITERS - 3)
+        pack_rim(other)
+        wait_rim(slot)
+        terms = [[(part, j, beta * value) for part, j, value in found] for found in along_terms(slot, rim, bond_edge)]
+        for side in range(2):
+            for part, j, value in terms[side]:
+                rim_send[other, 1 - side, spot(part, j)] += value
+        more = n < ITERS - 3
+
+        @pl.when(more)
         def _():
-            halo_send(other)
+            send_rim(other)
+
+        def put(part, r, at, value):
+            pull[part, r, at : at + 1, :] += value
+            field[other, part, 3 + r, PAD + at : PAD + at + 1, :] += value
+
+        spread(terms, put)
+
+        @pl.when(more)
+        def _():
+            send_all(other, across)
 
         advance(alpha, beta, slot)
         products(n + 2, other, False)
@@ -841,20 +1014,19 @@
         pltpu.VMEM((SLOTS, 2, 7, 8, DEPTH), F32),
         pltpu.VMEM((SLOTS, 4, 16, DEPTH), F32),
         pltpu.VMEM((4, TALL, WIDE, DEPTH), I32),
-        pltpu.VMEM((2, 4, 3, 8, DEPTH), I32),
+        pltpu.VMEM((2, 4, 3, WIDE, DEPTH), I32),
+        pltpu.VMEM((2, 4, 3, 24, DEPTH), I32),
         pltpu.VMEM((4, 16, DEPTH), I32),
         pltpu.VMEM((2, 4, 3, 8, DEPTH), I32),
         pltpu.VMEM((4, 16, DEPTH), I32),
         pltpu.VMEM((BONDS, ROWS * COLS, DEPTH), F32),
         pltpu.VMEM((2, len(EDGE), ROWS, DEPTH), F32),
         pltpu.VMEM((6, ROWS, COLS, DEPTH), F32),
-        pltpu.VMEM(block, F32),
-        pltpu.VMEM((2,) + block, F32),
-        pltpu.VMEM((2,) + block, F32),
+        pltpu.VMEM((4,) + block, F32),
         pltpu.VMEM(block, F32),
         pltpu.VMEM(block[1:], I32),
-        pltpu.VMEM((turns, nx, 8, DEPTH), F32),
-        pltpu.VMEM((turns, ny, 8, DEPTH), F32),
+        pltpu.VMEM((turns, nx, 1, DEPTH), F32),
+        pltpu.VMEM((turns, ny, 1, DEPTH), F32),
         dma((7,)),
         dma((SLOTS, 10)),
         dma((SLOTS, 10)),
@@ -865,12 +1037,12 @@
     ]
     return pl.pallas_call(
         functools.partial(kernel, nx, ny),
-        out_shape=[jax.ShapeDtypeStruct(block, F32)] * 2,
+        out_shape=[pltpu.VMEM(block, F32)] * 2,
         in_specs=[any_spec] * 5,
         out_specs=[vmem_spec] * 2,
         scratch_shapes=scratch,
         compiler_params=pltpu.CompilerParams(
-            collective_id=0, has_side_effects=True, vmem_limit_bytes=40 * 1024 * 1024
+            collective_id=0, has_side_effects=True, vmem_limit_bytes=60_000_000
         ),
     )(disp, vel, load, flags, mask_bits)
 

time: 75.8 us -> 64.2 us (0.85)
  Pallas kernels: 68.5 us -> 62.1 us
  local copies, waits for them, and re-layouts: 5.92 us -> 1.36 us
    pallas_call x1, Pallas kernels: 68.5 us -> 62.1 us  [on_device(): pl.pallas_call(functools.partial(kernel, nx, ny), out_shape=[pltpu.VMEM(b...]
    unnamed x12 -> x2, local copies, waits for them, and re-layouts: 5.92 us -> 1.36 us
where the time goes in v1:
time: 64.2 us; the launch traced here: 64.1 us
  Pallas kernels  62.1 us (97%)
  local copies, waits for them, and re-layouts  1.36 us (2%)
    pallas_call x1, Pallas kernels, on_device(): pl.pallas_call(functools.partial(kernel, nx, ny), out_shape=[pltpu.VMEM(b...  62.1 us
    unnamed x2, local copies, waits for them, and re-layouts  1.36 us

profile of v1, /device:TPU:0, one launch (start us, length us, event | category | flops | bytes accessed | tf_op | source)
XLA Modules:
  0.0 64.1 jit_solution(1262319509672835264)
XLA Ops:
  0.6 62.1 %shard_map.68 = (f32[3,8,16,128]{3,2,1,0:T(8,128)S(1)}, f32[3,8,16,128]{3,2,1,0:T(8,128)S(1)}) custom-call(f32[3,8,16,128]{3,2,1,0:T(8,128)} %disp.1, f32[3,8,16,128]{3,2,1,0:T(8,128)} %vel.1, f32[3,8,16,128]{3,2,1,0:T(8,128)} %load.1, s32[8,16,128]{2,1,0:T(8,128)} %flags.1, s32[4,8,16,128]{3,2,1,0:T(8,128)} %mask.1), custom_call_target="tpu_custom_call" | custom-call | tf_op jit(solution)/shard_map/pallas_call | solution.py:1038
  62.8 0.7 %copy.9 = f32[3,8,16,128]{3,2,1,0:T(8,128)} copy(f32[3,8,16,128]{3,2,1,0:T(8,128)S(1)} %get-tuple-element.2) | data formatting | bytes 393216
  63.4 0.7 %copy.10 = f32[3,8,16,128]{3,2,1,0:T(8,128)} copy(f32[3,8,16,128]{3,2,1,0:T(8,128)S(1)} %get-tuple-element.3) | data formatting | bytes 393216

commit v2 on v1

--- a/solution.py
+++ b/solution.py
@@ -528,7 +528,7 @@
 def kernel(
     nx, ny,
     disp, vel, load, flags, mask,
-    u_out, v_out,
+    u_out, v_out, t_out, a_out, b_out,
     field, near, far, rim, corner, rim_send, corner_send,
     words, words_near, words_rim, words_corner, words_rim_send, words_corner_send,
     bond, bond_edge, diag,
@@ -737,10 +737,26 @@
             n = into[dx] * 2 + into[dy]
             return [(words_corner_send.at[n], words_corner.at[n], 4 + n)]
         if dx:
-            first = 3 if dx < 0 else ROWS
-            return [(words.at[:, pl.ds(first, 3), own_cols], words_near.at[into[dx], :, :, own_cols], into[dx])]
+            side = into[dx]
+            first, third = edge_rows(dx)
+            two, one = (pl.ds(0, 2), 2) if side else (pl.ds(1, 2), 0)
+            w = third_word((3, 0, 0), side)
+            return [
+                (words.at[:, pl.ds(3 + first, 2), own_cols], words_near.at[side, :, two, own_cols], side),
+                (words.at[w, 3 + third, own_cols], words_near.at[side, w, one, own_cols], 8 + side),
+            ]
         side = into[dy]
-        return [(words_rim_send.at[side], words_rim.at[side, :, :, pl.ds(8, 8)], 2 + side)]
+        w = third_word((0, 3, 0), side)
+        two = pl.ds(0, 2)
+        return [
+            (words_rim_send.at[side, :, two], words_rim.at[side, :, two, pl.ds(8, 8)], 2 + side),
+            (words_rim_send.at[side, w, 2], words_rim.at[side, w, 2, pl.ds(8, 8)], 10 + side),
+        ]
+
+    def third_word(offset, side):
+        if not side:
+            offset = tuple(-part for part in offset)
+        return (BONDS - 1 - NUMBER[offset]) // 31
 
     def word_copy(dx, dy, src, dst, n):
         return pltpu.make_async_remote_copy(
@@ -766,12 +782,13 @@
         def _():
             for src, dst, n in word_copies(dx, dy):
                 word_copy(dx, dy, src, dst, n).start()
-    for n in range(2):
-        loads[2 - n].wait()
-        halo_send(n)
+    loads[2].wait()
+    halo_send(0)
 
     clear()
     build_bonds(words, bond, diag)
+    loads[1].wait()
+    halo_send(1)
     def words_wait():
         for dx, dy in sides:
             @pl.when(exists(dx, dy))
@@ -833,7 +850,7 @@
     def damping_of(turn, alpha, beta):
         g0, g1, g2, h0, h1, h2 = sum_end(turn)
         kinetic = alpha * alpha * g0 + 2.0 * alpha * beta * g1 + beta * beta * g2
-        rayleigh = -(alpha * alpha * h0 + alpha * beta * h1 + beta * beta * h2)
+        rayleigh = -(alpha * alpha * h0 + 2.0 * alpha * beta * h1 + beta * beta * h2)
         rayleigh = jnp.maximum(rayleigh, 0.0)
         damping = 2.0 * jnp.sqrt((rayleigh / count) / (MASS * (kinetic / count + EPSILON)))
         return (2.0 - damping) / (2.0 + damping), 2.0 / (MASS * (2.0 + damping))
@@ -843,24 +860,29 @@
 
     vregs = [(part, r, t) for part in range(3) for r in range(ROWS) for t in range(2)]
 
-    def products(turn, slot, first):
-        def body(r, carry):
-            acc = list(carry)
+    def tally_pair(acc, v, t, w):
+        return (acc[0] + v * v, acc[1] + v * t, acc[2] + t * t, acc[3] + v * w, acc[4] + t * w)
+
+    def early_products():
+        def body(r, acc):
             for part in range(3):
                 for t in range(2):
                     at = (part, r, pl.ds(8 * t, 8), slice(None))
-                    v, w = v_out[at], rate[at]
-                    acc[0] += v * v
-                    acc[3] += v * w
-                    if not first:
-                        tt, y = total[at], own(slot, part, r, t)
-                        acc[1] += v * tt
-                        acc[2] += tt * tt
-                        acc[4] += v * y + tt * w
-                        acc[5] += tt * y
+                    acc = tally_pair(acc, v_out[at], total[at], rate[at])
+            return acc
+
+        return lax.fori_loop(0, ROWS, body, (zero8,) * 5)
+
+    def late_product(slot):
+        def body(r, acc):
+            acc = list(acc)
+            for part in range(3):
+                for t in range(2):
+                    acc[t] = acc[t] + total[part, r, pl.ds(8 * t, 8), :] * own(slot, part, r, t)
             return tuple(acc)
 
-        sum_begin(turn, lax.fori_loop(0, ROWS, body, (zero8,) * 6))
+        acc = lax.fori_loop(0, ROWS, body, (zero8,) * 2)
+        return acc[0] + acc[1]
 
     def rest(slot, out):
         wait_all(slot, across)
@@ -907,32 +929,34 @@
 
         @pl.when(n == 1)
         def _():
-            products(0, 0, True)
+            sum_begin(0, early_products() + (zero8,))
 
         @pl.when(n == 2)
         def _():
             sum_middle(0)
-            products(1, 0, False)
+            sum_begin(1, early_products() + (late_product(0),))
 
         return carry
 
     lax.fori_loop(0, 4, begin, 0)
 
     def advance(alpha, beta, slot):
-        def body(r, carry):
+        def body(r, acc):
             for part in range(3):
                 for t in range(2):
                     at = (part, r, pl.ds(8 * t, 8), slice(None))
                     v, tt, w, y = v_out[at], total[at], rate[at], own(slot, part, r, t)
                     v = alpha * v + beta * tt
                     w = alpha * w + beta * y
+                    tt = tt + w
                     v_out[at] = v
                     u_out[at] = u_out[at] + v
                     rate[at] = w
-                    total[at] = tt + w
-            return carry
-
-        lax.fori_loop(0, ROWS, body, 0)
+                    total[at] = tt
+                    acc = tally_pair(acc, v, tt, w)
+            return acc
+
+        return lax.fori_loop(0, ROWS, body, (zero8,) * 5)
 
     def cycle(n, carry):
         alpha, beta = carry
@@ -955,6 +979,7 @@
 
         lax.fori_loop(0, ROWS, body, 0)
         pack_rim(other)
+        early = advance(alpha, beta, slot)
         wait_rim(slot)
         terms = [[(part, j, beta * value) for part, j, value in found] for found in along_terms(slot, rim, bond_edge)]
         for side in range(2):
@@ -971,32 +996,36 @@
             field[other, part, 3 + r, PAD + at : PAD + at + 1, :] += value
 
         spread(terms, put)
+        sum_begin(n + 2, early + (late_product(other),))
 
         @pl.when(more)
         def _():
             send_all(other, across)
 
-        advance(alpha, beta, slot)
-        products(n + 2, other, False)
         return alpha, beta
 
     one = jnp.ones((8, DEPTH), F32)
     alpha, beta = lax.fori_loop(0, ITERS - 2, cycle, (one, jnp.zeros((8, DEPTH), F32)))
     sum_middle(ITERS - 1)
     alpha, beta = damping_of(ITERS - 2, alpha, beta)
-    advance(alpha, beta, (ITERS - 2) % 2)
-    alpha, beta = damping_of(ITERS - 1, alpha, beta)
-
-    def finish(r, carry):
+    slot = (ITERS - 2) % 2
+
+    def last(r, carry):
         for part in range(3):
             for t in range(2):
                 at = (part, r, pl.ds(8 * t, 8), slice(None))
-                v = alpha * v_out[at] + beta * total[at]
+                v, tt = v_out[at], total[at]
+                v = alpha * v + beta * tt
                 v_out[at] = v
                 u_out[at] = u_out[at] + v
+                t_out[at] = tt + alpha * rate[at] + beta * own(slot, part, r, t)
         return carry
 
-    lax.fori_loop(0, ROWS, finish, 0)
+    lax.fori_loop(0, ROWS, last, 0)
+    alpha, beta = damping_of(ITERS - 1, alpha, beta)
+    for t in range(2):
+        a_out[8 * t : 8 * t + 8, :] = alpha
+        b_out[8 * t : 8 * t + 8, :] = beta
 
 
 def on_device(nx, ny, disp, vel, load, flags, mask_bits):
@@ -1030,21 +1059,23 @@
         dma((7,)),
         dma((SLOTS, 10)),
         dma((SLOTS, 10)),
-        dma((8,)),
-        dma((8,)),
+        dma((12,)),
+        dma((12,)),
         dma((2, turns)),
         dma((2, turns)),
     ]
-    return pl.pallas_call(
+    u, v, total, alpha, beta = pl.pallas_call(
         functools.partial(kernel, nx, ny),
-        out_shape=[pltpu.VMEM(block, F32)] * 2,
+        out_shape=[pltpu.VMEM(block, F32)] * 3 + [pltpu.VMEM(block[2:], F32)] * 2,
         in_specs=[any_spec] * 5,
-        out_specs=[vmem_spec] * 2,
+        out_specs=[vmem_spec] * 5,
         scratch_shapes=scratch,
         compiler_params=pltpu.CompilerParams(
             collective_id=0, has_side_effects=True, vmem_limit_bytes=60_000_000
         ),
     )(disp, vel, load, flags, mask_bits)
+    v = alpha * v + beta * total
+    return u + v, v
 
 
 def solution(mesh):

time: 64.2 us -> 62.7 us (0.977)
  local copies, waits for them, and re-layouts: 1.36 us -> 0 us
  Pallas kernels: 62.1 us -> 61.2 us
  other arithmetic: 0 us -> 0.78 us
    unnamed x2 -> x0, local copies, waits for them, and re-layouts: 1.36 us -> none
    pallas_call x1, Pallas kernels: 62.1 us -> 61.2 us  [on_device(): pl.pallas_call(functools.partial(kernel, nx, ny), out_shape=[pltpu.VMEM(b...]
    add x0 -> x1, other arithmetic: none -> 0.78 us  [on_device(): return (u + v, v)]
where the time goes in v2:
time: 62.7 us; the launch traced here: 62.6 us
  Pallas kernels  61.2 us (98%)
  other arithmetic  0.78 us (1%)
  between operations  0.64 us (1%)
    pallas_call x1, Pallas kernels, on_device(): pl.pallas_call(functools.partial(kernel, nx, ny), out_shape=[pltpu.VMEM(b...  61.2 us

profile of v2, /device:TPU:0, one launch (start us, length us, event | category | flops | bytes accessed | tf_op | source)
XLA Modules:
  0.0 62.6 jit_solution(6836511636186694202)
XLA Ops:
  0.6 61.2 %shard_map.68 = (f32[3,8,16,128]{3,2,1,0:T(8,128)S(1)}, f32[3,8,16,128]{3,2,1,0:T(8,128)S(1)}, f32[3,8,16,128]{3,2,1,0:T(8,128)S(1)}, f32[16,128]{1,0:T(8,128)S(1)}, f32[16,128]{1,0:T(8,128)S(1)}) custom-call(f32[3,8,16,128]{3,2,1,0:T(8,128)} %disp.1, f32[3,8,16,128]{3,2,1,0:T(8,128)} %vel.1, f32[3,8,16,128]{3,2,1,0:T(8,128)} %load.1, s32[8,16,128]{2,1,0:T(8,128)} %flags.1, ...), custom_call_target="tpu_custom_call" | custom-call | tf_op jit(solution)/shard_map/pallas_call | solution.py:1067
  61.8 0.8 %fusion = (f32[3,8,16,128]{3,2,1,0:T(8,128)}, f32[3,8,16,128]{3,2,1,0:T(8,128)}) fusion(f32[3,8,16,128]{3,2,1,0:T(8,128)S(1)} %get-tuple-element.7, f32[3,8,16,128]{3,2,1,0:T(8,128)S(1)} %get-tuple-element.11, f32[16,128]{1,0:T(8,128)S(1)} %get-tuple-element.10, f32[3,8,16,128]{3,2,1,0:T(8,128)S(1)} %get-tuple-element.9, f32[16,128]{1,0:T(8,128)S(1)} %get-tuple-element.8), kind=kLoop, calls=%fused_computation.1 | loop fusion | flops 196608 | bytes 999424 | tf_op jit(solution)/shard_map/add | solution.py:1078

commit v3 on v2

--- a/solution.py
+++ b/solution.py
@@ -17,7 +17,6 @@
 PAD = 8
 WIDE = COLS + 2 * PAD
 TALL = ROWS + 6
-GROUP = 4
 SLOTS = 4
 F32 = jnp.float32
 I32 = jnp.int32
@@ -105,6 +104,16 @@
     if factor == -2:
         return 2.0 * (total - value)
     return plus_scaled(total, factor, value)
+
+
+def accumulate_square(total, factor, value):
+    if factor == 0:
+        return total
+    if factor == 2:
+        return value
+    if factor == -2:
+        return 4.0 * (total + value)
+    return add(total, value)
 
 
 def turned(value, c):
@@ -132,81 +141,79 @@
 
 
 def local_pass(slot, field, bond, diag, out):
-    def group(g, carry):
-        base = g * GROUP
-        for t in range(2):
-            col = PAD + 8 * t
-
-            def coef(offset, i):
-                start = pl.multiple_of((base + i) * COLS + 8 * t, 8)
-                return bond[NUMBER[offset], pl.ds(start, 8), :]
-
-            def source(part, i, b):
-                return field[slot, part, base + 3 + i, pl.ds(col + b, 8), :]
-
-            for c in (0, 1, -1, 2, -2, 3, -3):
-                g0 = [None] * GROUP
-                g1 = [None] * GROUP
-                g2 = [None] * GROUP
-                if c:
-                    for i in range(GROUP):
-                        g2[i] = coef((0, 0, c), i) * source(2, i, 0)
-                if c == 0:
-                    for i in range(GROUP):
-                        for a in (1, -1, 2, -2, 3, -3):
+    for t in range(2):
+        col = PAD + 8 * t
+
+        def coef(offset, i):
+            start = i * COLS + 8 * t
+            return bond[NUMBER[offset], pl.ds(start, 8), :]
+
+        def source(part, i, b):
+            return field[slot, part, 3 + i, pl.ds(col + b, 8), :]
+
+        for c in (0, 1, -1, 2, -2, 3, -3):
+            g0 = [None] * ROWS
+            g1 = [None] * ROWS
+            g2 = [None] * ROWS
+            if c:
+                for i in range(ROWS):
+                    g2[i] = coef((0, 0, c), i) * source(2, i, 0)
+            if c == 0:
+                for i in range(ROWS):
+                    for a in (1, -1, 2, -2, 3, -3):
+                        if 0 <= i + a < ROWS:
                             g0[i] = add(g0[i], coef((a, 0, 0), i) * source(0, i + a, 0))
-                        for b in (1, -1, 2, -2, 3, -3):
-                            g1[i] = add(g1[i], coef((0, b, 0), i) * source(1, i, b))
-                if abs(c) < 3:
-                    n0 = [None] * GROUP
-                    n1 = [None] * GROUP
-                    for b in (2, -2, 1, -1, 0):
-                        reach = oblique(b, c)
-                        if not reach:
-                            continue
-                        span = range(min(reach), GROUP + max(reach))
-                        u0 = {i: source(0, i, b) for i in span}
-                        twice = {i: 2.0 * u0[i] for i in span} if 2 in reach else None
-                        u1 = {i: source(1, i, b) if b else None for i in span}
-                        u2 = {i: source(2, i, b) if c else None for i in span}
-                        s = {i: combine((b, c), (u1[i], u2[i])) for i in span}
-                        for i in range(GROUP):
-                            terms = {}
-                            for a in reach:
-                                near = s[i + a]
-                                if abs(a) == 1:
-                                    near = near + u0[i + a] if a > 0 else near - u0[i + a]
-                                elif a:
-                                    near = near + twice[i + a] if a > 0 else near - twice[i + a]
-                                terms[a] = coef((a, b, c), i) * near
-                            zeroth, first = moments(terms)
-                            g0[i] = add(g0[i], first)
-                            if c:
-                                n0[i] = add(n0[i], zeroth)
-                            if b == 2:
-                                n1[i] = zeroth
-                            elif b == -2:
-                                n1[i] = 2.0 * (n1[i] - zeroth)
-                            elif b:
-                                n1[i] = plus_scaled(n1[i], b, zeroth)
-                    for i in range(GROUP):
-                        g1[i] = add(g1[i], n1[i])
+                    for b in (1, -1, 2, -2, 3, -3):
+                        g1[i] = add(g1[i], coef((0, b, 0), i) * source(1, i, b))
+            if abs(c) < 3:
+                n0 = [None] * ROWS
+                n1 = [None] * ROWS
+                for b in (2, -2, 1, -1, 0):
+                    reach = oblique(b, c)
+                    if not reach:
+                        continue
+                    span = range(ROWS)
+                    u0 = {i: source(0, i, b) for i in span}
+                    twice = {i: 2.0 * u0[i] for i in span} if 2 in reach else None
+                    u1 = {i: source(1, i, b) if b else None for i in span}
+                    u2 = {i: source(2, i, b) if c else None for i in span}
+                    s = {i: combine((b, c), (u1[i], u2[i])) for i in span}
+                    for i in range(ROWS):
+                        terms = {}
+                        for a in reach:
+                            if not 0 <= i + a < ROWS:
+                                continue
+                            near = s[i + a]
+                            if abs(a) == 1:
+                                near = near + u0[i + a] if a > 0 else near - u0[i + a]
+                            elif a:
+                                near = near + twice[i + a] if a > 0 else near - twice[i + a]
+                            terms[a] = coef((a, b, c), i) * near
+                        zeroth, first = moments(terms)
+                        g0[i] = add(g0[i], first)
                         if c:
-                            g2[i] = plus_scaled(g2[i], c, n0[i])
-                for i in range(GROUP):
-                    for part, value in enumerate((g0[i], g1[i], g2[i])):
-                        if c == 0:
-                            if diag is not None:
-                                u = [source(other, i, 0) for other in range(3)]
-                                value = less_diagonal(value, diag, part, base + i, t, u)
-                            elif value is None:
-                                value = jnp.zeros((8, DEPTH), F32)
-                            out[part, base + i, pl.ds(8 * t, 8), :] = value
-                        elif value is not None:
-                            out[part, base + i, pl.ds(8 * t, 8), :] += turned(value, c)
-        return carry
-
-    lax.fori_loop(0, ROWS // GROUP, group, 0)
+                            n0[i] = add(n0[i], zeroth)
+                        if b == 2:
+                            n1[i] = zeroth
+                        elif b == -2:
+                            n1[i] = 2.0 * (n1[i] - zeroth)
+                        elif b:
+                            n1[i] = plus_scaled(n1[i], b, zeroth)
+                for i in range(ROWS):
+                    g1[i] = add(g1[i], n1[i])
+                    if c:
+                        g2[i] = plus_scaled(g2[i], c, n0[i])
+            for i in range(ROWS):
+                for part, value in enumerate((g0[i], g1[i], g2[i])):
+                    if c == 0:
+                        if diag is not None:
+                            u = [source(other, i, 0) for other in range(3)]
+                            value = less_diagonal(value, diag, part, i, t, u)
+                        elif value is None:
+                            value = jnp.zeros((8, DEPTH), F32)
+                        out[part, i, pl.ds(8 * t, 8), :] = value
+                    elif value is not None:
+                        out[part, i, pl.ds(8 * t, 8), :] += turned(value, c)
 
 
 def less_diagonal(value, diag, part, r, t, u):
@@ -415,7 +422,8 @@
             for c in range(-3, 4):
                 near = moved(own, c)
                 sums = [None] * 6
-                for b in range(-3, 4):
+                plain = up = twice = None
+                for b in (3, -3, 2, -2, 1, -1, 0):
                     values = {}
                     for a in range(-3, 4):
                         k = NUMBER.get((a, b, c))
@@ -439,14 +447,18 @@
                         second = 4.0 * (values[2] + values[-2])
                     second = add(second, values[1] + values[-1])
                     sums[0] = add(sums[0], second)
-                    if b:
-                        sums[1] = plus_scaled(sums[1], b, first)
-                        sums[2] = plus_scaled(sums[2], b * b, zeroth)
-                    if c:
-                        sums[3] = plus_scaled(sums[3], c, first)
-                        sums[5] = plus_scaled(sums[5], c * c, zeroth)
-                        if b:
-                            sums[4] = plus_scaled(sums[4], b * c, zeroth)
+                    sums[1] = accumulate_first(sums[1], b, first)
+                    sums[4] = accumulate_first(sums[4], b, zeroth)
+                    twice = accumulate_square(twice, b, zeroth)
+                    up = add(up, first)
+                    plain = add(plain, zeroth)
+                sums[2] = twice if sums[2] is None else (sums[2] if twice is None else sums[2] + twice)
+                if c and plain is not None:
+                    sums[3] = scaled(c, up)
+                    sums[5] = sums[5] + scaled(c * c, plain)
+                    sums[4] = scaled(c, sums[4])
+                else:
+                    sums[4] = None
                 for n in range(6):
                     if sums[n] is not None:
                         totals[n] = add(totals[n], turned(sums[n], c))
@@ -776,6 +788,7 @@
             for layer in range(2):
                 at = (w * 2 + layer) * 2
                 words_corner_send[n, at : at + 2, :] = words_rim_send[1 if dy < 0 else 0, w, layer, ends(dx), :]
+    clear()
     pl.semaphore_wait(barrier, nx + ny + 2)
     for dx, dy in sides:
         @pl.when(exists(dx, dy))
@@ -785,18 +798,24 @@
     loads[2].wait()
     halo_send(0)
 
-    clear()
     build_bonds(words, bond, diag)
     loads[1].wait()
     halo_send(1)
-    def words_wait():
-        for dx, dy in sides:
+    def words_wait(which):
+        for dx, dy in which:
             @pl.when(exists(dx, dy))
             def _():
                 for src, dst, n in word_copies(dx, dy):
                     word_copy(dx, dy, src, dst, n).wait_send()
                 for src, dst, n in word_copies(-dx, -dy):
                     word_copy(dx, dy, src, dst, n).wait_recv()
+
+    def words_across():
+        words_wait(across)
+        build_across(words, words_near, bond, diag)
+
+    def words_along():
+        words_wait(along + diagonals)
         for dx, dy in diagonals:
             sx, sy = (1 if dx > 0 else 0), (1 if dy > 0 else 0)
 
@@ -807,7 +826,6 @@
                         at = (w * 2 + layer) * 2
                         words_rim[sy, w, layer, beyond(dx), :] = words_corner[sx * 2 + sy, at : at + 2, :]
 
-        build_across(words, words_near, bond, diag)
         build_along(words_rim_send, words_rim, bond_edge, diag)
 
     def sum_copy(src, dst, which, turn, where):
@@ -884,9 +902,10 @@
         acc = lax.fori_loop(0, ROWS, body, (zero8,) * 2)
         return acc[0] + acc[1]
 
-    def rest(slot, out):
+    def rest(slot, out, meanwhile):
         wait_all(slot, across)
         across_pass(slot, near, far, bond, out)
+        meanwhile()
         wait_rim(slot)
 
         def put(part, r, at, value):
@@ -903,9 +922,14 @@
 
         @pl.when(n == 0)
         def _():
-            words_wait()
-
-        rest(n, out)
+            words_across()
+
+        def meanwhile():
+            @pl.when(n == 0)
+            def _():
+                words_along()
+
+        rest(n, out, meanwhile)
         loaded = lax.div(3 - n, 3).astype(F32)
         to = lax.rem(n + 2, 4)
 

time: 62.7 us -> 59.8 us (0.954)
  Pallas kernels: 61.2 us -> 58.3 us
    pallas_call x1, Pallas kernels: 61.2 us -> 58.3 us  [on_device(): pl.pallas_call(functools.partial(kernel, nx, ny), out_shape=[pltpu.VMEM(b...]
where the time goes in v3:
time: 59.8 us; the launch traced here: 59.7 us
  Pallas kernels  58.3 us (97%)
  other arithmetic  0.78 us (1%)
  between operations  0.64 us (1%)
    pallas_call x1, Pallas kernels, on_device(): pl.pallas_call(functools.partial(kernel, nx, ny), out_shape=[pltpu.VMEM(b...  58.3 us

profile of v3, /device:TPU:0, one launch (start us, length us, event | category | flops | bytes accessed | tf_op | source)
XLA Modules:
  0.0 59.7 jit_solution(1984654011974750896)
XLA Ops:
  0.6 58.3 %shard_map.68 = (f32[3,8,16,128]{3,2,1,0:T(8,128)S(1)}, f32[3,8,16,128]{3,2,1,0:T(8,128)S(1)}, f32[3,8,16,128]{3,2,1,0:T(8,128)S(1)}, f32[16,128]{1,0:T(8,128)S(1)}, f32[16,128]{1,0:T(8,128)S(1)}) custom-call(f32[3,8,16,128]{3,2,1,0:T(8,128)} %disp.1, f32[3,8,16,128]{3,2,1,0:T(8,128)} %vel.1, f32[3,8,16,128]{3,2,1,0:T(8,128)} %load.1, s32[8,16,128]{2,1,0:T(8,128)} %flags.1, ...), custom_call_target="tpu_custom_call" | custom-call | tf_op jit(solution)/shard_map/pallas_call | solution.py:1091
  58.9 0.8 %fusion = (f32[3,8,16,128]{3,2,1,0:T(8,128)}, f32[3,8,16,128]{3,2,1,0:T(8,128)}) fusion(f32[3,8,16,128]{3,2,1,0:T(8,128)S(1)} %get-tuple-element.7, f32[3,8,16,128]{3,2,1,0:T(8,128)S(1)} %get-tuple-element.11, f32[16,128]{1,0:T(8,128)S(1)} %get-tuple-element.10, f32[3,8,16,128]{3,2,1,0:T(8,128)S(1)} %get-tuple-element.9, f32[16,128]{1,0:T(8,128)S(1)} %get-tuple-element.8), kind=kLoop, calls=%fused_computation.1 | loop fusion | flops 196608 | bytes 999424 | tf_op jit(solution)/shard_map/add | solution.py:1102

commit v4 on v3

--- a/solution.py
+++ b/solution.py
@@ -697,7 +697,7 @@
 
     def copy_of(slot, dx, dy, src, dst, n):
         return pltpu.make_async_remote_copy(
-            src_ref=src, dst_ref=dst, send_sem=send_sem.at[slot, n], recv_sem=recv_sem.at[slot, n],
+            src_ref=src, dst_ref=dst, send_sem=send_sem.at[lax.rem(slot, 2), n], recv_sem=recv_sem.at[slot, n],
             device_id=device(dx, dy),
         )
 
@@ -789,6 +789,7 @@
                 at = (w * 2 + layer) * 2
                 words_corner_send[n, at : at + 2, :] = words_rim_send[1 if dy < 0 else 0, w, layer, ends(dx), :]
     clear()
+    build_bonds(words, bond, diag)
     pl.semaphore_wait(barrier, nx + ny + 2)
     for dx, dy in sides:
         @pl.when(exists(dx, dy))
@@ -798,7 +799,6 @@
     loads[2].wait()
     halo_send(0)
 
-    build_bonds(words, bond, diag)
     loads[1].wait()
     halo_send(1)
     def words_wait(which):
@@ -830,7 +830,7 @@
 
     def sum_copy(src, dst, which, turn, where):
         return pltpu.make_async_remote_copy(
-            src_ref=src, dst_ref=dst, send_sem=sum_send.at[which, turn], recv_sem=sum_recv.at[which, turn],
+            src_ref=src, dst_ref=dst, send_sem=sum_send.at[which, lax.rem(turn, 2)], recv_sem=sum_recv.at[which, turn],
             device_id=where,
         )
 
@@ -1003,7 +1003,6 @@
 
         lax.fori_loop(0, ROWS, body, 0)
         pack_rim(other)
-        early = advance(alpha, beta, slot)
         wait_rim(slot)
         terms = [[(part, j, beta * value) for part, j, value in found] for found in along_terms(slot, rim, bond_edge)]
         for side in range(2):
@@ -1020,6 +1019,7 @@
             field[other, part, 3 + r, PAD + at : PAD + at + 1, :] += value
 
         spread(terms, put)
+        early = advance(alpha, beta, slot)
         sum_begin(n + 2, early + (late_product(other),))
 
         @pl.when(more)
@@ -1081,11 +1081,11 @@
         pltpu.VMEM((turns, nx, 1, DEPTH), F32),
         pltpu.VMEM((turns, ny, 1, DEPTH), F32),
         dma((7,)),
-        dma((SLOTS, 10)),
+        dma((2, 10)),
         dma((SLOTS, 10)),
         dma((12,)),
         dma((12,)),
-        dma((2, turns)),
+        dma((2, 2)),
         dma((2, turns)),
     ]
     u, v, total, alpha, beta = pl.pallas_call(

time: 59.8 us -> 59.3 us (level)
  no operation moved by 1% of the time
where the time goes in v4:
time: 59.3 us; the launch traced here: 59.2 us
  Pallas kernels  57.8 us (97%)
  other arithmetic  0.78 us (1%)
  between operations  0.64 us (1%)
    pallas_call x1, Pallas kernels, on_device(): pl.pallas_call(functools.partial(kernel, nx, ny), out_shape=[pltpu.VMEM(b...  57.8 us

profile of v4, /device:TPU:0, one launch (start us, length us, event | category | flops | bytes accessed | tf_op | source)
XLA Modules:
  0.0 59.2 jit_solution(4284582257947189923)
XLA Ops:
  0.6 57.8 %shard_map.68 = (f32[3,8,16,128]{3,2,1,0:T(8,128)S(1)}, f32[3,8,16,128]{3,2,1,0:T(8,128)S(1)}, f32[3,8,16,128]{3,2,1,0:T(8,128)S(1)}, f32[16,128]{1,0:T(8,128)S(1)}, f32[16,128]{1,0:T(8,128)S(1)}) custom-call(f32[3,8,16,128]{3,2,1,0:T(8,128)} %disp.1, f32[3,8,16,128]{3,2,1,0:T(8,128)} %vel.1, f32[3,8,16,128]{3,2,1,0:T(8,128)} %load.1, s32[8,16,128]{2,1,0:T(8,128)} %flags.1, ...), custom_call_target="tpu_custom_call" | custom-call | tf_op jit(solution)/shard_map/pallas_call | solution.py:1091
  58.4 0.8 %fusion = (f32[3,8,16,128]{3,2,1,0:T(8,128)}, f32[3,8,16,128]{3,2,1,0:T(8,128)}) fusion(f32[3,8,16,128]{3,2,1,0:T(8,128)S(1)} %get-tuple-element.7, f32[3,8,16,128]{3,2,1,0:T(8,128)S(1)} %get-tuple-element.11, f32[16,128]{1,0:T(8,128)S(1)} %get-tuple-element.10, f32[3,8,16,128]{3,2,1,0:T(8,128)S(1)} %get-tuple-element.9, f32[16,128]{1,0:T(8,128)S(1)} %get-tuple-element.8), kind=kLoop, calls=%fused_computation.1 | loop fusion | flops 196608 | bytes 999424 | tf_op jit(solution)/shard_map/add | solution.py:1102
